TPU v7x, 512 devices: a whole 4x8x8 slice. The times are simulated.
512 devices in a mesh: dp: 64 (over z, y), tensor: 8 (over x, core).
Axes of the slice: x: 4, y: 8, z: 8, core: 2. Of those that a mesh axis runs over, the one named last changes fastest.
Arguments:
- gradient: bfloat16 [64, 512, 8192], P('dp', 'tensor'), may hold values from -110 to 110
- momentum: bfloat16 [64, 512, 8192], P('dp', 'tensor'), may hold values from -6 to 6
- indices: int32 [64, 8, 128, 32], P('dp', 'tensor'), may hold values from 0 to 4095, all different within a row
Outputs:
- new_momentum: bfloat16 [64, 512, 8192], P('dp', 'tensor')
- update: bfloat16 [512, 8192], P('tensor')
Inputs may be any that keep to these rules, and one draw needn't show every extreme that they name: The 32 indices of one span of one replica are distinct; index a * 64 + b names row frequency a and column frequency b.
All inputs are finite; a program needn't handle non-finite values.
Results may differ from a plain program's by a relative error of at most 0.0049.
Values may be sent and summed in bfloat16 or wider, within the bound.
No kernel may reach another device: no remote copies, remote signals or barrier semaphores. Data moves between devices by JAX's collectives and lax.ppermute only.
A program may use at most 64 MiB of HBM per device.

v0:
```python
import jax
import jax.numpy as jnp
from jax import lax
from jax.sharding import Mesh
from jax.sharding import PartitionSpec as P

BLOCK = 64
TENSOR = ("tensor_0", "tensor_1")
DP = ("dp_0", "dp_1")
DP_TENSOR = ("dp_0", "dp_1", "tensor_0", "tensor_1")


EPSILON = 1e-06
DECAY = 0.999


def one_axis_at_a_time(value, axes):
    for axis in axes:
        value = lax.psum(value, axis)
    return value


def laid_out(pieces, dim):
    pieces = jnp.moveaxis(pieces, 0, dim)
    shape = pieces.shape
    return pieces.reshape(*shape[:dim], shape[dim] * shape[dim + 1], *shape[dim + 2 :])


def from_everyone(value, axis):
    copies = jnp.broadcast_to(value, (lax.axis_size(axis), *value.shape))
    return lax.all_to_all(copies, axis, split_axis=0, concat_axis=0, tiled=True)


def gather_directly(value, axis, dim):
    return laid_out(from_everyone(value, axis), dim)


def dct_basis(block_edge):
    frequency = jnp.arange(block_edge, dtype=jnp.float32)[:, None]
    position = jnp.arange(block_edge, dtype=jnp.float32)[None, :]
    waves = jnp.cos(jnp.pi * (2.0 * position + 1.0) * frequency / (2.0 * block_edge))
    weights = jnp.where(frequency == 0.0, jnp.sqrt(1.0 / block_edge), jnp.sqrt(2.0 / block_edge))
    return waves * weights


def to_spans(slab, block_edge):
    height, columns = slab.shape
    shaped = slab.reshape(height // block_edge, block_edge, columns // block_edge, block_edge)
    return shaped.transpose(0, 2, 1, 3).reshape(-1, block_edge, block_edge)


def from_spans(blocks, height, columns):
    block_edge = blocks.shape[-1]
    shaped = blocks.reshape(height // block_edge, columns // block_edge, block_edge, block_edge)
    return shaped.transpose(0, 2, 1, 3).reshape(height, columns)


def inverse(spectra, cosines):
    return jnp.einsum("ka,ckl,lb->cab", cosines, spectra, cosines, precision=lax.Precision.HIGHEST)


def densify(shipped, chosen, block_edge):
    sources, number, selected = shipped.shape
    merged_values = shipped.transpose(1, 0, 2).reshape(number, sources * selected)
    merged_ids = chosen.transpose(1, 0, 2).reshape(number, sources * selected)
    levels = jnp.arange(block_edge, dtype=jnp.int32)[None, :, None]
    row_hits = jnp.where(
        (merged_ids // block_edge)[:, None, :] == levels,
        merged_values[:, None, :],
        jnp.zeros((), jnp.bfloat16),
    )
    col_hits = ((merged_ids % block_edge)[:, None, :] == levels).astype(jnp.bfloat16)
    return jnp.einsum("caj,cbj->cab", row_hits, col_hits, preferred_element_type=jnp.float32)


def local(gradient, momentum, indices):
    block_edge = BLOCK
    cosines = dct_basis(block_edge)
    precise = lax.Precision.HIGHEST
    height = gradient.shape[1]
    columns = gradient.shape[2]
    renewed = DECAY * momentum[0].astype(jnp.float32) + gradient[0].astype(jnp.float32)
    spectra = jnp.einsum(
        "ka,cab,lb->ckl", cosines, to_spans(renewed, block_edge), cosines, precision=precise
    )
    span_count = spectra.shape[0]
    chosen = indices[0].reshape(span_count, indices.shape[-1])
    levels = jnp.arange(block_edge, dtype=jnp.int32)[None, None, :]
    row_pick = ((chosen // block_edge)[:, :, None] == levels).astype(jnp.float32)
    col_pick = ((chosen % block_edge)[:, :, None] == levels).astype(jnp.float32)
    partial_value = jnp.einsum("cka,cab->ckb", row_pick, spectra, precision=precise)
    picked = jnp.sum(partial_value * col_pick, axis=2)
    marker = jnp.einsum("cka,ckb->cab", row_pick, col_pick, precision=precise)
    restored = inverse(spectra * marker, cosines)
    new_momentum = (renewed - from_spans(restored, height, columns)).astype(jnp.bfloat16)[None]
    values = picked.astype(jnp.bfloat16)
    element_total = height * columns * lax.axis_size(TENSOR)
    replicas = lax.axis_size(DP)
    owned_count = span_count // replicas
    outgoing = (
        values.reshape(replicas, owned_count, -1),
        chosen.reshape(replicas, owned_count, -1),
    )
    owned = inverse(
        densify(
            lax.all_to_all(outgoing[0], DP, split_axis=0, concat_axis=0, tiled=True),
            lax.all_to_all(outgoing[1], DP, split_axis=0, concat_axis=0, tiled=True),
            block_edge,
        ),
        cosines,
    )
    energy = one_axis_at_a_time(jnp.sum(owned * owned), DP_TENSOR)
    scaled = (owned / jnp.sqrt(energy / element_total + EPSILON)).astype(jnp.bfloat16)
    whole = gather_directly(scaled, DP, 0)
    update = from_spans(whole, height, columns)
    return (new_momentum, update)


def solution(mesh):
    split = Mesh(mesh.devices.reshape(8, 8, 4, 2), ("dp_0", "dp_1", "tensor_0", "tensor_1"))
    placed = (P(DP, TENSOR, None), P(DP, TENSOR, None), P(DP, TENSOR, None, None))
    return jax.shard_map(
        local,
        mesh=split,
        in_specs=placed,
        out_specs=(P(DP, TENSOR, None), P(TENSOR, None)),
        check_vma=False,
    )
```

profile of v0, /device:TPU:1, one launch (start us, length us, event | category | flops | bytes accessed | tf_op | source)
XLA Modules:
  0.0 180.7 jit_solution(11154151874710446193)
XLA Ops:
  2.5 3.0 %add.77 = f32[1,64,128,64]{3,2,1,0:T(8,128)} reshape(f32[1,64,8192]{2,1,0:T(8,128)S(1)} %convert_add_fusion) | data formatting | bytes 4194304 | tf_op jit(solution)/shard_map/add | solution.py:82
  5.5 3.5 %copy.36 = f32[128,64,64]{0,1,2:T(8,128)S(1)} copy(f32[128,64,64]{2,0,1:T(8,128)} %bitcast.70) | data formatting | bytes 4194304 | tf_op jit(solution)/shard_map/reshape | solution.py:49
  9.2 4.3 %fusion.6 = f32[128,64,64]{2,1,0:T(8,128)} fusion(s32[128,32]{1,0:T(8,128)S(1)} %copy.39, s32[128,32]{1,0:T(8,128)S(1)} %copy.38), kind=kOutput, calls=%fused_computation.9 | convolution fusion | flops 34078720 | bytes 2129920 | tf_op jit(solution)/shard_map/cka,ckb->cab/dot_general | solution.py:93
  13.6 4.8 %copy.40 = f32[128,64,64]{0,2,1:T(8,128)} copy(f32[128,64,64]{2,1,0:T(8,128)} %fusion.6) | data formatting | bytes 4194304 | tf_op jit(solution)/shard_map/cka,ckb->cab/dot_general | solution.py:93
  20.6 4.7 %fusion.58 = (f32[128,64,64]{0,2,1:T(8,128)S(1)}, f32[128,64,64]{0,2,1:T(8,128)}) fusion(f32[128,64,64]{0,2,1:T(8,128)S(1)} %copy-done, f32[64]{0:T(128)S(1)} %get-tuple-element.10, f32[64]{0:T(128)S(1)} %get-tuple-element.11, f32[128,64,64]{0,2,1:T(8,128)S(1)} %fusion.28), kind=kOutput, calls=%fused_computation.81 | convolution fusion | flops 403189760 | bytes 8389120 | tf_op jit(solution)/shard_map/ka,cab,lb->ckl/dot_general | solution.py:83
  25.3 5.6 %copy.48 = f32[128,64,64]{2,1,0:T(8,128)} copy(f32[128,64,64]{0,2,1:T(8,128)} %get-tuple-element.7) | data formatting | bytes 4194304 | tf_op jit(solution)/shard_map/ka,cab,lb->ckl/dot_general | solution.py:83
  30.9 5.8 %select_reduce_fusion = bf16[128,32]{1,0:T(8,128)(2,1)} fusion(f32[128,64,64]{2,1,0:T(8,128)} %copy.48, s32[128,32]{1,0:T(8,128)S(1)} %copy.39, s32[128,32]{1,0:T(8,128)S(1)} %copy.38), kind=kOutput, calls=%fused_computation.6 | convolution fusion | flops 202371072 | bytes 2138112 | tf_op jit(solution)/shard_map/cka,cab->ckb/dot_general | solution.py:91
  36.7 17.3 %all-to-all-start.1 = ((bf16[64,2,32]{2,1,0:T(2,128)(2,1)}), bf16[64,2,32]{2,1,0:T(2,128)(2,1)S(1)}, u32[]{:S(2)}, u32[]{:S(2)}) async-start(bf16[64,2,32]{2,1,0:T(2,128)(2,1)} %bitcast.10), calls=%async_computation.1 | async-start | bytes 65536 | tf_op jit(solution)/shard_map/all_to_all | solution.py:106
  54.7 10.1 %all-to-all-done.1 = bf16[64,2,32]{2,1,0:T(2,128)(2,1)S(1)} async-done(((bf16[64,2,32]{2,1,0:T(2,128)(2,1)}), bf16[64,2,32]{2,1,0:T(2,128)(2,1)S(1)}, u32[]{:S(2)}, u32[]{:S(2)}) %all-to-all-start.1) | async-done | bytes 8224 | tf_op jit(solution)/shard_map/all_to_all | solution.py:106
  64.8 4.6 %all-to-all-start = ((s32[64,2,32]{2,1,0:T(2,128)}), s32[64,2,32]{2,1,0:T(2,128)S(1)}, u32[]{:S(2)}, u32[]{:S(2)}) async-start(s32[64,2,32]{2,1,0:T(2,128)} %bitcast.8), calls=%async_computation | async-start | bytes 131072 | tf_op jit(solution)/shard_map/all_to_all | solution.py:107
  69.5 11.0 %all-to-all-done = s32[64,2,32]{2,1,0:T(2,128)S(1)} async-done(((s32[64,2,32]{2,1,0:T(2,128)}), s32[64,2,32]{2,1,0:T(2,128)S(1)}, u32[]{:S(2)}, u32[]{:S(2)}) %all-to-all-start) | async-done | bytes 16416 | tf_op jit(solution)/shard_map/all_to_all | solution.py:107
  82.4 11.8 %psum.28 = f32[]{:T(128)} all-reduce(f32[]{:T(128)} %get-tuple-element.8), channel_id=1, replica_groups=mesh['dp_0'=8,'dp_1'=8,'tensor_0'=4,'tensor_1'=2] {'dp_0'}, use_global_device_ids=true, to_apply=%region_2.3 | all-reduce | flops 1 | bytes 8 | tf_op jit(solution)/shard_map/psum | solution.py:19
  94.2 11.7 %psum.29 = f32[]{:T(128)} all-reduce(f32[]{:T(128)} %psum.28), channel_id=1, replica_groups=mesh['dp_0'=8,'dp_1'=8,'tensor_0'=4,'tensor_1'=2] {'dp_1'}, use_global_device_ids=true, to_apply=%region_3.4 | all-reduce | flops 1 | bytes 8 | tf_op jit(solution)/shard_map/psum | solution.py:19
  106.0 9.1 %psum.30 = f32[]{:T(128)} all-reduce(f32[]{:T(128)} %psum.29), channel_id=1, replica_groups=mesh['dp_0'=8,'dp_1'=8,'tensor_0'=4,'tensor_1'=2] {'tensor_0'}, use_global_device_ids=true, to_apply=%region_4.5 | all-reduce | flops 1 | bytes 8 | tf_op jit(solution)/shard_map/psum | solution.py:19
  115.0 4.8 %fusion.2 = f32[128,64,64]{0,2,1:T(8,128)} fusion(f32[128,64,64]{0,2,1:T(8,128)S(1)} %get-tuple-element.6, f32[64]{0:T(128)S(1)} %get-tuple-element.10, f32[64]{0:T(128)S(1)} %get-tuple-element.11), kind=kOutput, calls=%fused_computation.2 | convolution fusion | flops 402665472 | bytes 4194816 | tf_op jit(solution)/shard_map/ka,ckl,lb->cab/dot_general | solution.py:59
  119.8 15.3 %psum.31 = f32[]{:T(128)} all-reduce(f32[]{:T(128)} %psum.30), channel_id=1, replica_groups=mesh['dp_0'=8,'dp_1'=8,'tensor_0'=4,'tensor_1'=2] {'tensor_1'}, use_global_device_ids=true, to_apply=%region_5.6 | all-reduce | flops 1 | bytes 8 | tf_op jit(solution)/shard_map/psum | solution.py:19
  137.9 2.3 %reshape.178 = bf16[64,2,4096]{2,1,0:T(2,128)(2,1)} reshape(bf16[64,64,2,64]{3,2,1,0:T(2,128)(2,1)S(1)} %broadcast_bitcast_fusion) | data formatting | bytes 2097152
  140.2 7.2 %all-to-all-start.2 = ((bf16[64,2,4096]{2,1,0:T(2,128)(2,1)}), bf16[64,2,4096]{2,1,0:T(2,128)(2,1)S(1)}, u32[]{:S(2)}, u32[]{:S(2)}) async-start(bf16[64,2,4096]{2,1,0:T(2,128)(2,1)} %reshape.178), calls=%async_computation.2 | async-start | bytes 2097152 | tf_op jit(solution)/shard_map/all_to_all | solution.py:31
  147.3 4.9 %fusion.8 = f32[1,64,128,64]{2,3,1,0:T(8,128)S(1)} fusion(f32[128,64,64]{0,2,1:T(8,128)} %fusion.2, f32[64]{0:T(128)S(1)} %get-tuple-element.10, f32[64]{0:T(128)S(1)} %get-tuple-element.11), kind=kOutput, calls=%fused_computation.13 | convolution fusion | flops 402665472 | bytes 4194816 | tf_op jit(solution)/shard_map/ka,ckl,lb->cab/dot_general | solution.py:59
  152.2 2.7 %copy.45 = f32[1,64,128,64]{3,2,1,0:T(8,128)} copy(f32[1,64,128,64]{2,3,1,0:T(8,128)S(1)} %fusion.8) | data formatting | bytes 4194304 | tf_op jit(solution)/shard_map/transpose | solution.py:55
  154.9 3.5 %reshape.172 = f32[1,64,8192]{2,1,0:T(8,128)S(1)} reshape(f32[1,64,128,64]{3,2,1,0:T(8,128)} %copy.45) | data formatting | bytes 4194304 | tf_op jit(solution)/shard_map/reshape | solution.py:55
  158.4 2.9 %subtract_convert_fusion = bf16[1,64,8192]{2,1,0:T(8,128)(2,1)} fusion(f32[1,64,8192]{2,1,0:T(8,128)S(1)} %reshape.172, bf16[1,64,8192]{2,1,0:T(8,128)(2,1)} %param.3, bf16[1,64,8192]{2,1,0:T(8,128)(2,1)} %param.4), kind=kLoop, calls=%fused_computation.7 | loop fusion | flops 3145728 | bytes 5242880 | tf_op jit(solution)/shard_map/convert_element_type | solution.py:95
  161.3 13.6 %all-to-all-done.2 = bf16[64,2,4096]{2,1,0:T(2,128)(2,1)S(1)} async-done(((bf16[64,2,4096]{2,1,0:T(2,128)(2,1)}), bf16[64,2,4096]{2,1,0:T(2,128)(2,1)S(1)}, u32[]{:S(2)}, u32[]{:S(2)}) %all-to-all-start.2) | async-done | bytes 1048608 | tf_op jit(solution)/shard_map/all_to_all | solution.py:31
  178.3 2.5 %reshape.174 = bf16[64,8192]{1,0:T(8,128)(2,1)} reshape(bf16[1,64,128,64]{3,2,1,0:T(8,128)(2,1)S(1)} %copy.54) | data formatting | bytes 2097152 | tf_op jit(solution)/shard_map/reshape | solution.py:55
  (25 shorter events, 12.2 us)
Async XLA Ops:
  5.5 3.5 %copy-start.1 = (s32[1,1,128,32]{2,3,1,0:T(8,128)S(1)}, s32[1,1,128,32]{2,3,1,0:T(8,128)}, u32[]{:S(2)}) copy-start(s32[1,1,128,32]{2,3,1,0:T(8,128)} %param.5) | copy-start | bytes 49156
  18.4 2.2 %copy-start = (f32[128,64,64]{0,2,1:T(8,128)S(1)}, f32[128,64,64]{0,2,1:T(8,128)}, u32[]{:S(2)}) copy-start(f32[128,64,64]{0,2,1:T(8,128)} %copy.40) | copy-start | bytes 6291460
  36.7 28.1 %all-to-all-start.1 = ((bf16[64,2,32]{2,1,0:T(2,128)(2,1)}), bf16[64,2,32]{2,1,0:T(2,128)(2,1)S(1)}, u32[]{:S(2)}, u32[]{:S(2)}) async-start(bf16[64,2,32]{2,1,0:T(2,128)(2,1)} %bitcast.10), calls=%async_computation.1 | async-start | bytes 65536 | tf_op jit(solution)/shard_map/all_to_all | solution.py:106
  64.8 15.7 %all-to-all-start = ((s32[64,2,32]{2,1,0:T(2,128)}), s32[64,2,32]{2,1,0:T(2,128)S(1)}, u32[]{:S(2)}, u32[]{:S(2)}) async-start(s32[64,2,32]{2,1,0:T(2,128)} %bitcast.8), calls=%async_computation | async-start | bytes 131072 | tf_op jit(solution)/shard_map/all_to_all | solution.py:107
  140.2 34.8 %all-to-all-start.2 = ((bf16[64,2,4096]{2,1,0:T(2,128)(2,1)}), bf16[64,2,4096]{2,1,0:T(2,128)(2,1)S(1)}, u32[]{:S(2)}, u32[]{:S(2)}) async-start(bf16[64,2,4096]{2,1,0:T(2,128)(2,1)} %reshape.178), calls=%async_computation.2 | async-start | bytes 2097152 | tf_op jit(solution)/shard_map/all_to_all | solution.py:31
where the time goes:
time: 182 us; the launch traced here: 181 us
  blocking collectives  48 us (26%)
  waiting for transfers between devices  34.7 us (19%)
  local copies, waits for them, and re-layouts  34.4 us (19%)
  starting transfers between devices  29.1 us (16%)
  matrix products  28.4 us (16%)
  other arithmetic  4.81 us (3%)
    psum x4, blocking collectives, one_axis_at_a_time(): value = lax.psum(value, axis)  48 us
    all_to_all x1, starting transfers between devices, local(): lax.all_to_all(outgoing[0], DP, split_axis=0, concat_axis=0, tiled=True)  17.3 us
    all_to_all x1, waiting for transfers between devices, from_everyone(): return lax.all_to_all(copies, axis, split_axis=0, concat_axis=0, tiled=True)  13.6 us
    dot_general x4, matrix products, inverse(): jnp.einsum('ka,ckl,lb->cab', cosines, spectra, cosines, precision=lax.Pre...  11 us
    all_to_all x1, waiting for transfers between devices, local(): lax.all_to_all(outgoing[1], DP, split_axis=0, concat_axis=0, tiled=True)  11 us
    all_to_all x1, waiting for transfers between devices, local(): lax.all_to_all(outgoing[0], DP, split_axis=0, concat_axis=0, tiled=True)  10.1 us
    all_to_all x1, starting transfers between devices, from_everyone(): return lax.all_to_all(copies, axis, split_axis=0, concat_axis=0, tiled=True)  7.17 us
    dot_general x2, matrix products, local(): jnp.einsum('ka,cab,lb->ckl', cosines, to_spans(renewed, block_edge), cosi...  6.91 us
  transfers between devices with their start and end apart: 3, of which 3 were waited for; matrix products, arithmetic and copies ran while one was open for 8% of the time, Pallas kernels for 0%

commit v1 on v0

v1 whole, which is shorter than its diff:
```python
import functools

import jax
import jax.numpy as jnp
import numpy as np
from jax import lax
from jax.experimental import pallas as pl
from jax.experimental.pallas import tpu as pltpu
from jax.sharding import Mesh
from jax.sharding import PartitionSpec as P

BLOCK = 64
LANES = 256
QUAD = 4
TENSOR = ("tensor_0", "tensor_1")
DP = ("dp_0", "dp_1")

EPSILON = 1e-06
DECAY = 0.999
F32 = jnp.float32
BF16 = jnp.bfloat16


def dct_basis():
    frequency = np.arange(BLOCK, dtype=np.float64)[:, None]
    position = np.arange(BLOCK, dtype=np.float64)[None, :]
    waves = np.cos(np.pi * (2.0 * position + 1.0) * frequency / (2.0 * BLOCK))
    return (waves * np.where(frequency == 0.0, np.sqrt(1.0 / BLOCK), np.sqrt(2.0 / BLOCK))).astype(np.float32)


def constant_halves(x):
    high = x.astype(BF16)
    return high, (x - high.astype(np.float32)).astype(BF16)


def from_left(cosines):
    high, low = constant_halves(cosines)
    return jnp.asarray(np.concatenate([high, high, low], axis=1))


def from_right(cosines):
    return jnp.asarray(np.stack(constant_halves(np.kron(np.eye(QUAD, dtype=np.float32), cosines))))


def halves(x):
    high = x.astype(BF16)
    return high, (x - high.astype(F32)).astype(BF16)


def dot(a, b):
    return lax.dot_general(a, b, (((1,), (0,)), ((), ())), preferred_element_type=F32)


def dot_t(a, b):
    return lax.dot_general(a, b, (((1,), (1,)), ((), ())), preferred_element_type=F32)


def times_right(tiles, right_ref):
    high, low = halves(tiles)
    return dot(high, right_ref[0]) + dot(low, right_ref[0]) + dot(high, right_ref[1])


def times_left(left_ref, tile):
    high, low = halves(tile)
    return dot(left_ref[...], jnp.concatenate([high, low, high], axis=0))


def spread_rows(index_row, tile_lanes=LANES):
    count = index_row.shape[1]
    per_span = count // QUAD
    span = lax.broadcasted_iota(jnp.int32, (1, count), 1) // per_span
    row = (index_row // BLOCK).astype(F32).astype(BF16)
    col = ((index_row % BLOCK) + span * BLOCK).astype(F32).astype(BF16)
    row_levels = lax.broadcasted_iota(jnp.int32, (BLOCK, count), 0).astype(F32).astype(BF16)
    col_levels = lax.broadcasted_iota(jnp.int32, (tile_lanes, count), 0).astype(F32).astype(BF16)
    return row_levels == row, col_levels == col


def spectra(gradient_ref, momentum_ref, right_ref, left_ref, tiles):
    cuts = [slice(t * LANES, (t + 1) * LANES) for t in range(tiles)]
    renewed = [DECAY * momentum_ref[:, c].astype(F32) + gradient_ref[:, c].astype(F32) for c in cuts]
    half = times_right(jnp.concatenate(renewed, axis=0), right_ref)
    return renewed, [times_left(left_ref, half[t * BLOCK : (t + 1) * BLOCK]) for t in range(tiles)]


def pick_kernel(tiles, peers, gradient_ref, momentum_ref, index_ref, right_ref, left_ref, out_ref, picked_ref):
    step = pl.program_id(0)
    _, spectrum = spectra(gradient_ref, momentum_ref, right_ref, left_ref, tiles)
    rows = []
    for t in range(tiles):
        index_row = index_ref[pl.ds(step * tiles + t, 1), :]
        row_hit, col_hit = spread_rows(index_row)
        by_col = dot(spectrum[t].astype(BF16), jnp.where(col_hit, 1.0, 0.0).astype(BF16))
        rows.append(jnp.sum(jnp.where(row_hit, by_col, 0.0), axis=0, keepdims=True))
    picked_ref[pl.ds(pl.multiple_of(step * tiles, tiles), tiles), :] = jnp.concatenate(rows, axis=0)

    @pl.when(step == pl.num_programs(0) - 1)
    def _():
        index = index_ref[...]
        row = index // BLOCK
        scale = jnp.ones(index.shape, F32)
        for bit in range(6):
            scale = jnp.where((row >> bit) & 1 == 1, scale * float(2 ** (2**bit)), scale)
        coded = (BLOCK + index % BLOCK).astype(F32) * scale
        groups, count = index.shape
        selected = count // QUAD
        spans = groups * QUAD
        group_of = lax.broadcasted_iota(jnp.int32, (groups, spans), 1) // QUAD
        copy_group = jnp.where(lax.broadcasted_iota(jnp.int32, (groups, spans), 0) == group_of, 1.0, 0.0).astype(BF16)
        lane = lax.broadcasted_iota(jnp.int32, (count, spans), 0)
        keep = lane // selected == lax.broadcasted_iota(jnp.int32, (count, spans), 1) % QUAD
        lane_of = lax.broadcasted_iota(jnp.int32, (selected, count), 1) % selected
        gather_lane = jnp.where(lax.broadcasted_iota(jnp.int32, (selected, count), 0) == lane_of, 1.0, 0.0).astype(BF16)
        parts = []
        for table in (picked_ref[...], coded):
            spread = dot(jnp.transpose(table).astype(BF16), copy_group)
            parts.append(dot(gather_lane, jnp.where(keep, spread, 0.0).astype(BF16)))
        payload = jnp.concatenate(parts, axis=0).astype(BF16)
        for peer in range(peers):
            out_ref[peer] = payload


def pick(gradient, momentum, index_rows, right, left, peers, steps=4):
    height, columns = gradient.shape
    width = columns // steps
    tiles = width // LANES
    groups, count = index_rows.shape
    selected, spans = count // QUAD, groups * QUAD
    slab = pl.BlockSpec((height, width), lambda i: (0, i))
    whole = lambda shape: pl.BlockSpec(shape, lambda i: (0,) * len(shape))
    return pl.pallas_call(
        functools.partial(pick_kernel, tiles, peers),
        grid=(steps,),
        in_specs=[slab, slab, whole(index_rows.shape), whole(right.shape), whole(left.shape)],
        out_specs=whole((peers, 2 * selected, spans)),
        out_shape=jax.ShapeDtypeStruct((peers, 2 * selected, spans), BF16),
        scratch_shapes=[pltpu.VMEM((groups, count), F32)],
        name="pick",
    )(gradient, momentum, index_rows, right, left)


def remain_kernel(tiles, gradient_ref, momentum_ref, index_ref, right_ref, left_ref, back_right_ref, back_left_ref, out_ref):
    step = pl.program_id(0)
    renewed, spectrum = spectra(gradient_ref, momentum_ref, right_ref, left_ref, tiles)
    kept = []
    for t in range(tiles):
        index_row = index_ref[pl.ds(step * tiles + t, 1), :]
        row_hit, col_hit = spread_rows(index_row)
        one = lambda hit: jnp.where(hit, 1.0, 0.0).astype(BF16)
        marker = dot_t(one(row_hit), one(col_hit))
        kept.append(spectrum[t] * marker)
    half = times_right(jnp.concatenate(kept, axis=0), back_right_ref)
    for t in range(tiles):
        restored = times_left(back_left_ref, half[t * BLOCK : (t + 1) * BLOCK])
        out_ref[:, t * LANES : (t + 1) * LANES] = (renewed[t] - restored).astype(BF16)


def remain(gradient, momentum, index_rows, right, left, back_right, back_left, steps=4):
    height, columns = gradient.shape
    width = columns // steps
    tiles = width // LANES
    slab = pl.BlockSpec((height, width), lambda i: (0, i))
    whole = lambda shape: pl.BlockSpec(shape, lambda i: (0,) * len(shape))
    return pl.pallas_call(
        functools.partial(remain_kernel, tiles),
        grid=(steps,),
        in_specs=[slab, slab] + [whole(a.shape) for a in (index_rows, right, left, back_right, back_left)],
        out_specs=slab,
        out_shape=jax.ShapeDtypeStruct((height, columns), BF16),
        name="remain",
        cost_estimate=pl.CostEstimate(flops=5_000_000_000, bytes_accessed=6 * height * columns, transcendentals=0),
    )(gradient, momentum, index_rows, right, left, back_right, back_left)


CHUNK = 256
UNROLL = 4


def decode_kernel(in_ref, back_right_ref, back_left_ref, after_ref, decoded_ref, energy_ref, value_ref, row_ref, col_ref, sum_ref):
    sources, double, spans = in_ref.shape
    selected = double // 2
    entries = sources * selected
    per = CHUNK // selected
    for c in range(0, entries, CHUNK):
        s = c // selected
        values = jnp.concatenate([in_ref[s + i, :selected, :] for i in range(per)], axis=0)
        code = jnp.concatenate([in_ref[s + i, selected:, :] for i in range(per)], axis=0)
        row = jnp.zeros(code.shape, BF16)
        for shift in (32, 16, 8, 4, 2, 1):
            above = code >= jnp.asarray(BLOCK * 2.0**shift, BF16)
            code = jnp.where(above, code * jnp.asarray(2.0**-shift, BF16), code)
            row = jnp.where(above, row + jnp.asarray(shift, BF16), row)
        value_ref[:, c : c + CHUNK] = jnp.transpose(values.astype(F32))
        row_ref[:, c : c + CHUNK] = jnp.transpose(row.astype(F32))
        col_ref[:, c : c + CHUNK] = jnp.transpose(code.astype(F32) - float(BLOCK))
    levels = lax.broadcasted_iota(jnp.int32, (BLOCK, CHUNK), 0).astype(F32).astype(BF16)
    zero = jnp.zeros((BLOCK, CHUNK), BF16)
    one = jnp.ones((BLOCK, CHUNK), BF16)

    def combine(span):
        total = None
        for c in range(0, entries, CHUNK):
            part = (pl.ds(span, 1), slice(c, c + CHUNK))
            value, row, col = (ref[part].astype(BF16) for ref in (value_ref, row_ref, col_ref))
            by_row = jnp.where(levels == row, jnp.broadcast_to(value, (BLOCK, CHUNK)), zero)
            by_col = jnp.where(levels == col, one, zero)
            term = dot_t(by_row, by_col)
            total = term if total is None else total + term
        return total

    def body(i, energy):
        for u in range(UNROLL):
            tile = i * UNROLL + u
            parts = [combine(tile * QUAD + k) for k in range(QUAD)]
            for p in parts:
                square = p * p
                for r in range(0, BLOCK, 8):
                    energy = energy + square[r : r + 8]
            sum_ref[pl.ds(pl.multiple_of(tile * BLOCK, BLOCK), BLOCK), :] = jnp.concatenate(parts, axis=1)
        return energy

    tiles = spans // QUAD
    energy = lax.fori_loop(0, tiles // UNROLL, body, jnp.zeros((8, BLOCK), F32))
    energy = jnp.concatenate([energy, jnp.zeros_like(energy)], axis=1)
    for peer in range(energy_ref.shape[0]):
        energy_ref[peer] = energy
    batch = 8
    for first in range(0, tiles, batch):
        half = times_right(sum_ref[first * BLOCK : (first + batch) * BLOCK, :], back_right_ref)
        for t in range(batch):
            tile = times_left(back_left_ref, half[t * BLOCK : (t + 1) * BLOCK])
            decoded_ref[:, (first + t) * LANES : (first + t + 1) * LANES] = tile


def decode(received, back_right, back_left, after, rows):
    sources, double, spans = received.shape
    entries = sources * double // 2
    vmem = pl.BlockSpec(memory_space=pltpu.VMEM)
    return pl.pallas_call(
        decode_kernel,
        in_specs=[vmem] * 3 + [pl.BlockSpec(memory_space=pl.ANY)],
        out_specs=[vmem] * 2,
        out_shape=[
            pltpu.VMEM((BLOCK, spans * BLOCK), F32),
            jax.ShapeDtypeStruct((rows, 8, 128), F32),
        ],
        scratch_shapes=[pltpu.VMEM((spans, entries), F32)] * 3 + [pltpu.VMEM((spans // QUAD * BLOCK, LANES), F32)],
        name="decode",
    )(received, back_right, back_left, after)


def scale_kernel(count, decoded_ref, energy_ref, out_ref):
    total = jnp.sum(energy_ref[...], axis=0)
    total = jnp.sum(jnp.sum(total, axis=0, keepdims=True), axis=1, keepdims=True)
    factor = lax.rsqrt(total * (1.0 / count) + EPSILON)
    out_ref[...] = (decoded_ref[...] * factor).astype(BF16)


def scale(decoded, energies, count):
    vmem = pl.BlockSpec(memory_space=pltpu.VMEM)
    return pl.pallas_call(
        functools.partial(scale_kernel, count),
        in_specs=[vmem] * 2,
        out_specs=vmem,
        out_shape=jax.ShapeDtypeStruct(decoded.shape, BF16),
        name="scale",
    )(decoded, energies)


def in_vmem(x):
    return pltpu.with_memory_space_constraint(x, pltpu.VMEM)


def local(gradient, momentum, indices):
    gradient, momentum = gradient[0], momentum[0]
    height, columns = gradient.shape
    cosines = dct_basis()
    right, left = from_right(cosines.T), from_left(cosines)
    back_right, back_left = from_right(cosines), from_left(cosines.T)
    spans, selected = indices.shape[-2:]
    index_rows = indices.reshape(spans // QUAD, QUAD * selected)
    replicas, rows = lax.axis_size(DP), lax.axis_size(TENSOR)
    outgoing = pick(gradient, momentum, index_rows, right, left, replicas)
    received = lax.all_to_all(outgoing, DP, split_axis=0, concat_axis=0, tiled=True)
    new_momentum = remain(gradient, momentum, index_rows, right, left, back_right, back_left)
    decoded, energy = decode(in_vmem(received), back_right, back_left, new_momentum, rows)
    energies = lax.all_to_all(energy, TENSOR, split_axis=0, concat_axis=0, tiled=True)
    update = scale(in_vmem(decoded), in_vmem(energies), height * columns * rows)
    return (new_momentum[None], update)


def solution(mesh):
    split = Mesh(mesh.devices.reshape(8, 8, 4, 2), ("dp_0", "dp_1", "tensor_0", "tensor_1"))
    placed = (P(DP, TENSOR, None), P(DP, TENSOR, None), P(DP, TENSOR, None, None))
    return jax.shard_map(
        local,
        mesh=split,
        in_specs=placed,
        out_specs=(P(DP, TENSOR, None), P(TENSOR, None)),
        check_vma=False,
    )
```

time: 182 us -> 85.4 us (0.47)
  blocking collectives: 48 us -> 12.2 us
  Pallas kernels: 0 us -> 31.8 us
  local copies, waits for them, and re-layouts: 34.4 us -> 4.41 us
  matrix products: 28.4 us -> 0 us
  waiting for transfers between devices: 34.7 us -> 18.7 us
  starting transfers between devices: 29.1 us -> 17.1 us
  other arithmetic: 4.81 us -> 0 us
    psum x4 -> x0, blocking collectives: 48 us -> none  [one_axis_at_a_time(): value = lax.psum(value, axis)]
    pallas_call x0 -> x4, Pallas kernels: none -> 31.8 us  [the longest x1 15.3 us: decode(): pl.pallas_call(decode_kernel, in_specs=[vmem] * 3 + [pl.BlockSpec(memory_...]
    dot_general x9 -> x0, matrix products: 28.4 us -> none  [the longest x4 11 us: inverse(): jnp.einsum('ka,ckl,lb->cab', cosines, spectra, cosines, precision=lax.Pre...]
    all_to_all x3 -> x1, waiting for transfers between devices: 34.7 us -> 18.7 us  [local(): lax.all_to_all(outgoing, DP, split_axis=0, concat_axis=0, tiled=True)]
    all_to_all x0 -> x1, blocking collectives: none -> 12.2 us  [local(): lax.all_to_all(energy, TENSOR, split_axis=0, concat_axis=0, tiled=True)]
    all_to_all x3 -> x1, starting transfers between devices: 29.1 us -> 17.1 us  [local(): lax.all_to_all(outgoing, DP, split_axis=0, concat_axis=0, tiled=True)]
    dot_general x2 -> x0, local copies, waits for them, and re-layouts: 10.4 us -> none  [the longest x1 5.57 us: local(): jnp.einsum('ka,cab,lb->ckl', cosines, to_spans(renewed, block_edge), cosi...]
    reshape x4 -> x1, local copies, waits for them, and re-layouts: 9.64 us -> 0.68 us  [local(): index_rows = indices.reshape(spans // QUAD, QUAD * selected)]
  transfers between devices with their start and end apart: 3 -> 1, of which waited for: 3 -> 1; matrix products, arithmetic and copies ran while one was open for 8% -> 0% of each run, Pallas kernels for 0% -> 10%
where the time goes in v1:
time: 85.4 us; the launch traced here: 85 us
  Pallas kernels  31.8 us (37%)
  waiting for transfers between devices  18.7 us (22%)
  starting transfers between devices  17.1 us (20%)
  blocking collectives  12.2 us (14%)
  local copies, waits for them, and re-layouts  4.41 us (5%)
    all_to_all x1, waiting for transfers between devices, local(): lax.all_to_all(outgoing, DP, split_axis=0, concat_axis=0, tiled=True)  18.7 us
    all_to_all x1, starting transfers between devices, local(): lax.all_to_all(outgoing, DP, split_axis=0, concat_axis=0, tiled=True)  17.1 us
    pallas_call x1, Pallas kernels, decode(): pl.pallas_call(decode_kernel, in_specs=[vmem] * 3 + [pl.BlockSpec(memory_...  15.3 us
    all_to_all x1, blocking collectives, local(): lax.all_to_all(energy, TENSOR, split_axis=0, concat_axis=0, tiled=True)  12.2 us
    pallas_call x1, Pallas kernels, remain(): pl.pallas_call(functools.partial(remain_kernel, tiles), grid=(steps,), in...  8.75 us
    pallas_call x1, Pallas kernels, pick(): pl.pallas_call(functools.partial(pick_kernel, tiles, peers), grid=(steps,...  6.54 us
    unnamed x5, local copies, waits for them, and re-layouts  3.73 us
  transfers between devices with their start and end apart: 1, of which 1 were waited for; matrix products, arithmetic and copies ran while one was open for 0% of the time, Pallas kernels for 10%

profile of v1, /device:TPU:1, one launch (start us, length us, event | category | flops | bytes accessed | tf_op | source)
XLA Modules:
  0.0 85.0 jit_solution(17680822103250529460)
XLA Ops:
  0.6 0.8 copy.10
  1.4 0.7 reshape.7.index_ref
  2.1 6.5 %pick.1 = bf16[64,64,128]{2,1,0:T(8,128)(2,1)} custom-call(bf16[64,8192]{1,0:T(8,128)(2,1)} %bitcast.6, bf16[64,8192]{1,0:T(8,128)(2,1)} %bitcast.8, s32[32,128]{1,0:T(8,128)} %reshape.7.index_ref, bf16[2,256,256]{2,1,0:T(8,128)(2,1)} %constant.8.clone.right_ref, bf16[64,192]{1,0:T(8,128)(2,1)} %constant.9.clone.left_ref), custom_call_target="tpu_custom_call" | custom-call | tf_op jit(solution)/shard_map/pick/pallas_call | solution.py:131
  8.7 17.1 %all-to-all-start = ((bf16[64,64,128]{2,1,0:T(8,128)(2,1)}), bf16[64,64,128]{2,1,0:T(8,128)(2,1)S(1)}, u32[]{:S(2)}, u32[]{:S(2)}) async-start(bf16[64,64,128]{2,1,0:T(8,128)(2,1)} %pick.1), calls=%async_computation | async-start | bytes 2097152 | tf_op jit(solution)/shard_map/all_to_all | solution.py:284
  25.8 8.7 %remain.1.after_ref = bf16[64,8192]{1,0:T(8,128)(2,1)} custom-call(bf16[64,8192]{1,0:T(8,128)(2,1)} %bitcast.7, bf16[64,8192]{1,0:T(8,128)(2,1)} %bitcast.9, s32[32,128]{1,0:T(8,128)} %reshape.7.index_ref, bf16[2,256,256]{2,1,0:T(8,128)(2,1)} %constant.8.clone.right_ref, bf16[64,192]{1,0:T(8,128)(2,1)} %constant.9.clone.left_ref, ...), custom_call_target="tpu_custom_call" | custom-call | flops 5000000000 | bytes 3145728 | tf_op jit(solution)/shard_map/remain/pallas_call | solution.py:164
  34.5 18.7 %all-to-all-done.in_ref = bf16[64,64,128]{2,1,0:T(8,128)(2,1)S(1)} async-done(((bf16[64,64,128]{2,1,0:T(8,128)(2,1)}), bf16[64,64,128]{2,1,0:T(8,128)(2,1)S(1)}, u32[]{:S(2)}, u32[]{:S(2)}) %all-to-all-start) | async-done | bytes 1048608 | tf_op jit(solution)/shard_map/all_to_all | solution.py:284
  53.3 15.3 %decode.1 = (f32[64,8192]{1,0:T(8,128)S(1)}, f32[8,8,128]{2,1,0:T(8,128)}) custom-call(bf16[64,64,128]{2,1,0:T(8,128)(2,1)S(1)} %all-to-all-done.in_ref, bf16[2,256,256]{2,1,0:T(8,128)(2,1)} %constant.10.clone.back_right_ref, bf16[64,192]{1,0:T(8,128)(2,1)} %constant.11.clone.back_left_ref, bf16[64,8192]{1,0:T(8,128)(2,1)} %remain.1.after_ref), custom_call_target="tpu_custom_call" | custom-call | tf_op jit(solution)/shard_map/decode/pallas_call | solution.py:239
  68.5 0.0 copy-start
  68.5 1.3 %copy-done = f32[64,8192]{1,0:T(8,128)} copy-done((f32[64,8192]{1,0:T(8,128)}, f32[64,8192]{1,0:T(8,128)S(1)}, u32[]{:S(2)}) %copy-start) | copy-done | bytes 2097176
  69.9 12.2 %all_to_all.10.energy_ref = f32[8,8,128]{2,1,0:T(8,128)S(1)} all-to-all(f32[8,8,128]{2,1,0:T(8,128)} %get-tuple-element.5), channel_id=1, replica_groups=mesh['dp_0'=8,'dp_1'=8,'tensor_0'=4,'tensor_1'=2] {'tensor_0','tensor_1'}, dimensions={0} | all-to-all | bytes 65536 | tf_op jit(solution)/shard_map/all_to_all | solution.py:287
  82.1 0.0 copy-start.1
  82.1 1.6 %copy-done.1 = f32[64,8192]{1,0:T(8,128)S(1)} copy-done((f32[64,8192]{1,0:T(8,128)S(1)}, f32[64,8192]{1,0:T(8,128)}, u32[]{:S(2)}) %copy-start.1) | copy-done | bytes 2097176
  83.7 1.3 %scale.1 = bf16[64,8192]{1,0:T(8,128)(2,1)} custom-call(f32[64,8192]{1,0:T(8,128)S(1)} %copy-done.1, f32[8,8,128]{2,1,0:T(8,128)S(1)} %all_to_all.10.energy_ref), custom_call_target="tpu_custom_call" | custom-call | tf_op jit(solution)/shard_map/scale/pallas_call | solution.py:261
Async XLA Ops:
  8.7 44.6 %all-to-all-start = ((bf16[64,64,128]{2,1,0:T(8,128)(2,1)}), bf16[64,64,128]{2,1,0:T(8,128)(2,1)S(1)}, u32[]{:S(2)}, u32[]{:S(2)}) async-start(bf16[64,64,128]{2,1,0:T(8,128)(2,1)} %pick.1), calls=%async_computation | async-start | bytes 2097152 | tf_op jit(solution)/shard_map/all_to_all | solution.py:284
  68.5 1.3 %copy-start = (f32[64,8192]{1,0:T(8,128)}, f32[64,8192]{1,0:T(8,128)S(1)}, u32[]{:S(2)}) copy-start(f32[64,8192]{1,0:T(8,128)S(1)} %get-tuple-element.4.decoded_ref) | copy-start | bytes 6291460
  82.1 1.6 %copy-start.1 = (f32[64,8192]{1,0:T(8,128)S(1)}, f32[64,8192]{1,0:T(8,128)}, u32[]{:S(2)}) copy-start(f32[64,8192]{1,0:T(8,128)} %copy-done) | copy-start | bytes 6291460

commit v2 on v1

v2 whole, which is shorter than its diff:
```python
import functools

import jax
import jax.numpy as jnp
import numpy as np
from jax import lax
from jax.experimental import pallas as pl
from jax.experimental.pallas import tpu as pltpu
from jax.sharding import Mesh
from jax.sharding import PartitionSpec as P

BLOCK = 64
LANES = 256
QUAD = 4
TENSOR = ("tensor_0", "tensor_1")
DP = ("dp_0", "dp_1")

EPSILON = 1e-06
DECAY = 0.999
F32 = jnp.float32
BF16 = jnp.bfloat16


def dct_basis():
    frequency = np.arange(BLOCK, dtype=np.float64)[:, None]
    position = np.arange(BLOCK, dtype=np.float64)[None, :]
    waves = np.cos(np.pi * (2.0 * position + 1.0) * frequency / (2.0 * BLOCK))
    return (waves * np.where(frequency == 0.0, np.sqrt(1.0 / BLOCK), np.sqrt(2.0 / BLOCK))).astype(np.float32)


def constant_halves(x):
    high = x.astype(BF16)
    return high, (x - high.astype(np.float32)).astype(BF16)


def from_left(cosines):
    high, low = constant_halves(cosines)
    return jnp.asarray(np.concatenate([high, high, low], axis=1))


def from_right(cosines):
    return jnp.asarray(np.stack(constant_halves(np.kron(np.eye(QUAD, dtype=np.float32), cosines))))


def halves(x):
    high = x.astype(BF16)
    return high, (x - high.astype(F32)).astype(BF16)


def dot(a, b):
    return lax.dot_general(a, b, (((1,), (0,)), ((), ())), preferred_element_type=F32)


def dot_t(a, b):
    return lax.dot_general(a, b, (((1,), (1,)), ((), ())), preferred_element_type=F32)


def times_right(tiles, right_ref):
    high, low = halves(tiles)
    return dot(high, right_ref[0]) + dot(low, right_ref[0]) + dot(high, right_ref[1])


def times_left(left_ref, tile):
    high, low = halves(tile)
    return dot(left_ref[...], jnp.concatenate([high, low, high], axis=0))


def iota(shape, dim, kind=F32):
    return lax.broadcasted_iota(jnp.int32, shape, dim).astype(kind)


def hot(hit):
    return jnp.where(hit, jnp.ones(hit.shape, BF16), jnp.zeros(hit.shape, BF16))


def one_hot(hit):
    return jnp.where(hit, 1.0, 0.0).astype(BF16)


def col_hits(rows_ref, group, groups):
    col = rows_ref[pl.ds(groups + group, 1), :].astype(BF16)
    return hot(iota((LANES, col.shape[1]), 0).astype(BF16) == col)


def row_levels(rows_ref, group):
    row = rows_ref[pl.ds(group, 1), :]
    return row, iota((BLOCK, row.shape[1]), 0)


def spectra(gradient_ref, momentum_ref, right_ref, left_ref, tiles, first=0):
    cuts = [slice((first + t) * LANES, (first + t + 1) * LANES) for t in range(tiles)]
    renewed = [DECAY * momentum_ref[:, c].astype(F32) + gradient_ref[:, c].astype(F32) for c in cuts]
    half = times_right(jnp.concatenate(renewed, axis=0), right_ref)
    return renewed, [times_left(left_ref, half[t * BLOCK : (t + 1) * BLOCK]) for t in range(tiles)]


def lay_rows(index, rows_ref):
    selected, spans = index.shape
    groups, count = spans // QUAD, selected * QUAD
    copies = one_hot(iota((selected, count), 0, jnp.int32) == iota((selected, count), 1, jnp.int32) % selected)
    keep = iota((spans, count), 0, jnp.int32) % QUAD == iota((spans, count), 1, jnp.int32) // selected
    collect = one_hot(iota((groups, spans), 0, jnp.int32) == iota((groups, spans), 1, jnp.int32) // QUAD)
    span_start = (iota((1, count), 1, jnp.int32) // selected * BLOCK).astype(F32)
    for part, table in enumerate((index // BLOCK, index % BLOCK)):
        turned = jnp.transpose(table.astype(F32)).astype(BF16)
        laid = dot(collect, jnp.where(keep, dot(turned, copies), 0.0).astype(BF16))
        rows_ref[part * groups : (part + 1) * groups, :] = laid + span_start if part else laid


def lay_spans(picked):
    groups, count = picked.shape
    spans, selected = groups * QUAD, count // QUAD
    copies = one_hot(iota((groups, spans), 0, jnp.int32) == iota((groups, spans), 1, jnp.int32) // QUAD)
    keep = iota((count, spans), 0, jnp.int32) // selected == iota((count, spans), 1, jnp.int32) % QUAD
    collect = one_hot(iota((selected, count), 0, jnp.int32) == iota((selected, count), 1, jnp.int32) % selected)
    spread = dot(jnp.transpose(picked).astype(BF16), copies)
    return dot(collect, jnp.where(keep, spread, 0.0).astype(BF16))


def pick_kernel(
    steps, gradient_in, momentum_in, index_in, right_in, left_in, out_ref, rows_ref,
    gradient_ref, momentum_ref, index_ref, right_ref, left_ref, payload_ref, loaded, sent
):
    width = gradient_ref.shape[1] // steps
    tiles = width // LANES
    tables = [
        pltpu.make_async_copy(source, target, loaded.at[2 * steps + k])
        for k, (source, target) in enumerate(((index_in, index_ref), (right_in, right_ref), (left_in, left_ref)))
    ]
    loads = []
    for step in range(steps):
        part = (slice(None), pl.ds(step * width, width))
        loads.append(
            [
                pltpu.make_async_copy(source.at[part], target.at[part], loaded.at[2 * step + k])
                for k, (source, target) in enumerate(((gradient_in, gradient_ref), (momentum_in, momentum_ref)))
            ]
        )
    for group in [tables, *loads]:
        for load in group:
            load.start()
    tables[0].wait()
    index = index_ref[...]
    groups = index.shape[1] // QUAD
    lay_rows(index, rows_ref)
    rows = []
    for load in tables[1:]:
        load.wait()
    for step in range(steps):
        for load in loads[step]:
            load.wait()
        _, spectrum = spectra(gradient_ref, momentum_ref, right_ref, left_ref, tiles, step * tiles)
        for t in range(tiles):
            by_col = dot(spectrum[t].astype(BF16), col_hits(rows_ref, step * tiles + t, groups))
            row, levels = row_levels(rows_ref, step * tiles + t)
            rows.append(jnp.sum(jnp.where(levels == row, by_col, 0.0), axis=0, keepdims=True))
    row = index // BLOCK
    scale = jnp.ones(index.shape, F32)
    for bit in range(6):
        scale = jnp.where((row >> bit) & 1 == 1, scale * float(2 ** (2**bit)), scale)
    coded = (BLOCK + index % BLOCK).astype(F32) * scale
    payload_ref[...] = jnp.concatenate([lay_spans(jnp.concatenate(rows, axis=0)), coded], axis=0).astype(BF16)
    for peer in range(out_ref.shape[0]):
        pltpu.make_async_copy(payload_ref, out_ref.at[peer], sent).start()
    pltpu.make_async_copy(out_ref, out_ref, sent).wait()


VMEM = pl.BlockSpec(memory_space=pltpu.VMEM)
HBM = pl.BlockSpec(memory_space=pltpu.HBM)


def whole(shape):
    return pl.BlockSpec(shape, lambda i: (0,) * len(shape))


def pick(gradient, momentum, index, right, left, peers, steps=2):
    selected, spans = index.shape
    return pl.pallas_call(
        functools.partial(pick_kernel, steps),
        in_specs=[HBM] * 5,
        out_specs=[HBM, VMEM],
        out_shape=[
            pltpu.HBM((peers, 2 * selected, spans), BF16),
            pltpu.VMEM((2 * spans // QUAD, selected * QUAD), F32),
        ],
        scratch_shapes=[
            pltpu.VMEM(gradient.shape, BF16),
            pltpu.VMEM(momentum.shape, BF16),
            pltpu.VMEM(index.shape, jnp.int32),
            pltpu.VMEM(right.shape, BF16),
            pltpu.VMEM(left.shape, BF16),
            pltpu.VMEM((2 * selected, spans), BF16),
            pltpu.SemaphoreType.DMA((2 * steps + 3,)),
            pltpu.SemaphoreType.DMA,
        ],
        name="pick",
    )(gradient, momentum, index, right, left)


def remain_kernel(tiles, gradient_ref, momentum_ref, rows_ref, right_ref, left_ref, back_right_ref, back_left_ref, out_ref):
    step = pl.program_id(0)
    groups = rows_ref.shape[0] // 2
    renewed, spectrum = spectra(gradient_ref, momentum_ref, right_ref, left_ref, tiles)
    kept = []
    for t in range(tiles):
        row, levels = row_levels(rows_ref, step * tiles + t)
        marker = dot_t(hot(levels.astype(BF16) == row.astype(BF16)), col_hits(rows_ref, step * tiles + t, groups))
        kept.append(spectrum[t] * marker)
    half = times_right(jnp.concatenate(kept, axis=0), back_right_ref)
    for t in range(tiles):
        restored = times_left(back_left_ref, half[t * BLOCK : (t + 1) * BLOCK])
        out_ref[:, t * LANES : (t + 1) * LANES] = (renewed[t] - restored).astype(BF16)


def remain(gradient, momentum, rows, right, left, back_right, back_left, steps=4):
    height, columns = gradient.shape
    width = columns // steps
    slab = pl.BlockSpec((height, width), lambda i: (0, i))
    return pl.pallas_call(
        functools.partial(remain_kernel, width // LANES),
        grid=(steps,),
        in_specs=[slab, slab, VMEM] + [whole(a.shape) for a in (right, left, back_right, back_left)],
        out_specs=slab,
        out_shape=jax.ShapeDtypeStruct((height, columns), BF16),
        name="remain",
        cost_estimate=pl.CostEstimate(flops=5_000_000_000, bytes_accessed=6 * height * columns, transcendentals=0),
    )(gradient, momentum, rows, right, left, back_right, back_left)


CHUNK = 256
UNROLL = 4


def combine_kernel(in_ref, after_ref, out_ref, energy_out, value_ref, row_ref, col_ref, sum_ref, energy_ref, stored, shared):
    sources, double, spans = in_ref.shape
    selected = double // 2
    entries = sources * selected
    per = CHUNK // selected
    for c in range(0, entries, CHUNK):
        s = c // selected
        values = jnp.concatenate([in_ref[s + i, :selected, :] for i in range(per)], axis=0)
        code = jnp.concatenate([in_ref[s + i, selected:, :] for i in range(per)], axis=0)
        row = jnp.zeros(code.shape, BF16)
        for shift in (32, 16, 8, 4, 2, 1):
            above = code >= jnp.asarray(BLOCK * 2.0**shift, BF16)
            code = jnp.where(above, code * jnp.asarray(2.0**-shift, BF16), code)
            row = jnp.where(above, row + jnp.asarray(shift, BF16), row)
        value_ref[:, c : c + CHUNK] = jnp.transpose(values.astype(F32))
        row_ref[:, c : c + CHUNK] = jnp.transpose(row.astype(F32))
        col_ref[:, c : c + CHUNK] = jnp.transpose(code.astype(F32) - float(BLOCK))
    levels = lax.broadcasted_iota(jnp.int32, (BLOCK, CHUNK), 0).astype(F32).astype(BF16)
    zero = jnp.zeros((BLOCK, CHUNK), BF16)
    one = jnp.ones((BLOCK, CHUNK), BF16)

    def add_up(span):
        total = None
        for c in range(0, entries, CHUNK):
            part = (pl.ds(span, 1), slice(c, c + CHUNK))
            value, row, col = (ref[part].astype(BF16) for ref in (value_ref, row_ref, col_ref))
            by_row = jnp.where(levels == row, jnp.broadcast_to(value, (BLOCK, CHUNK)), zero)
            by_col = jnp.where(levels == col, one, zero)
            term = dot_t(by_row, by_col)
            total = term if total is None else total + term
        return total

    def body(i, energy):
        for u in range(UNROLL):
            tile = i * UNROLL + u
            parts = [add_up(tile * QUAD + k) for k in range(QUAD)]
            for p in parts:
                square = p * p
                for r in range(0, BLOCK, 8):
                    energy = energy + square[r : r + 8]
            sum_ref[pl.ds(pl.multiple_of(tile * BLOCK, BLOCK), BLOCK), :] = jnp.concatenate(parts, axis=1)
        part = pl.ds(pl.multiple_of(i * (UNROLL * BLOCK), UNROLL * BLOCK), UNROLL * BLOCK)
        pltpu.make_async_copy(sum_ref.at[part], out_ref.at[part], stored).start()
        return energy

    tiles = spans // QUAD
    energy = lax.fori_loop(0, tiles // UNROLL, body, jnp.zeros((8, BLOCK), F32))
    energy = jnp.concatenate([energy, jnp.zeros_like(energy)], axis=1)
    for peer in range(energy_ref.shape[0]):
        energy_ref[peer] = energy
    share = pltpu.make_async_copy(energy_ref, energy_out, shared)
    share.start()
    pltpu.make_async_copy(sum_ref, out_ref, stored).wait()
    share.wait()


def combine(received, after, rows):
    sources, double, spans = received.shape
    entries = sources * double // 2
    return pl.pallas_call(
        combine_kernel,
        in_specs=[VMEM, HBM],
        out_specs=[HBM, HBM],
        out_shape=[pltpu.HBM((spans // QUAD * BLOCK, LANES), F32), pltpu.HBM((rows, 8, 128), F32)],
        scratch_shapes=[pltpu.VMEM((spans, entries), F32)] * 3
        + [pltpu.VMEM((spans // QUAD * BLOCK, LANES), F32), pltpu.VMEM((rows, 8, 128), F32)]
        + [pltpu.SemaphoreType.DMA] * 2,
        name="combine",
    )(received, after)


def decode_kernel(steps, sum_in, right_ref, left_ref, out_ref, sum_ref, loaded):
    height = sum_ref.shape[0] // steps
    loads = []
    for step in range(steps):
        part = pl.ds(step * height, height)
        loads.append(pltpu.make_async_copy(sum_in.at[part], sum_ref.at[part], loaded.at[step]))
    for load in loads:
        load.start()
    for step in range(steps):
        loads[step].wait()
        half = times_right(sum_ref[step * height : (step + 1) * height, :], right_ref)
        for t in range(height // BLOCK):
            lane = (step * (height // BLOCK) + t) * LANES
            out_ref[:, lane : lane + LANES] = times_left(left_ref, half[t * BLOCK : (t + 1) * BLOCK])


def decode(sums, right, left, steps=4):
    tiles = sums.shape[0] // BLOCK
    return pl.pallas_call(
        functools.partial(decode_kernel, steps),
        in_specs=[HBM, VMEM, VMEM],
        out_specs=VMEM,
        out_shape=pltpu.VMEM((BLOCK, tiles * LANES), F32),
        scratch_shapes=[pltpu.VMEM(sums.shape, F32), pltpu.SemaphoreType.DMA((steps,))],
        compiler_params=pltpu.CompilerParams(vmem_limit_bytes=24 * 2**20),
        name="decode",
        cost_estimate=pl.CostEstimate(flops=2_000_000_000, bytes_accessed=8 * sums.size, transcendentals=0),
    )(sums, right, left)


def scale_kernel(steps, count, decoded_ref, energy_ref, out_ref, scaled_ref, stored):
    total = jnp.sum(energy_ref[...], axis=0)
    total = jnp.sum(jnp.sum(total, axis=0, keepdims=True), axis=1, keepdims=True)
    factor = lax.rsqrt(total * (1.0 / count) + EPSILON)
    width = out_ref.shape[1] // steps
    stores = []
    for step in range(steps):
        part = (slice(None), pl.ds(step * width, width))
        scaled_ref[part] = (decoded_ref[part] * factor).astype(BF16)
        stores.append(pltpu.make_async_copy(scaled_ref.at[part], out_ref.at[part], stored.at[step]))
        stores[-1].start()
    for store in stores:
        store.wait()


def scale(decoded, energies, count, steps=4):
    return pl.pallas_call(
        functools.partial(scale_kernel, steps, count),
        in_specs=[VMEM, VMEM],
        out_specs=HBM,
        out_shape=pltpu.HBM(decoded.shape, BF16),
        scratch_shapes=[pltpu.VMEM(decoded.shape, BF16), pltpu.SemaphoreType.DMA((steps,))],
        compiler_params=pltpu.CompilerParams(vmem_limit_bytes=24 * 2**20),
        name="scale",
    )(decoded, energies)


def in_vmem(x):
    return pltpu.with_memory_space_constraint(x, pltpu.VMEM)


def in_hbm(x):
    return pltpu.with_memory_space_constraint(x, pltpu.HBM)


def local(gradient, momentum, indices):
    gradient, momentum = in_hbm(gradient[0]), in_hbm(momentum[0])
    height, columns = gradient.shape
    cosines = dct_basis()
    right, left = from_right(cosines.T), from_left(cosines)
    back_right, back_left = from_right(cosines), from_left(cosines.T)
    index = indices.reshape(indices.shape[-2:]).T
    replicas, rows = lax.axis_size(DP), lax.axis_size(TENSOR)
    outgoing, index_rows = pick(gradient, momentum, in_hbm(index), in_hbm(right), in_hbm(left), replicas)
    received = lax.all_to_all(outgoing, DP, split_axis=0, concat_axis=0, tiled=True)
    new_momentum = remain(gradient, momentum, index_rows, right, left, back_right, back_left)
    sums, energy = combine(in_vmem(received), in_hbm(new_momentum), rows)
    energies = lax.all_to_all(energy, TENSOR, split_axis=0, concat_axis=0, tiled=True)
    decoded = decode(in_hbm(sums), in_vmem(back_right), in_vmem(back_left))
    update = scale(in_vmem(decoded), in_vmem(energies), height * columns * rows)
    return (new_momentum[None], update)


def solution(mesh):
    split = Mesh(mesh.devices.reshape(8, 8, 4, 2), ("dp_0", "dp_1", "tensor_0", "tensor_1"))
    placed = (P(DP, TENSOR, None), P(DP, TENSOR, None), P(DP, TENSOR, None, None))
    return jax.shard_map(
        local,
        mesh=split,
        in_specs=placed,
        out_specs=(P(DP, TENSOR, None), P(TENSOR, None)),
        check_vma=False,
    )
```

time: 85.4 us -> 77 us (0.902)
  blocking collectives: 12.2 us -> 0 us
  starting transfers between devices: 17.1 us -> 24.7 us
  local copies, waits for them, and re-layouts: 4.41 us -> 0.01 us
    all_to_all x1 -> x0, blocking collectives: 12.2 us -> none  [local(): lax.all_to_all(energy, TENSOR, split_axis=0, concat_axis=0, tiled=True)]
    all_to_all x0 -> x1, starting transfers between devices: none -> 7.54 us  [local(): lax.all_to_all(energy, TENSOR, split_axis=0, concat_axis=0, tiled=True)]
    unnamed x5 -> x6, local copies, waits for them, and re-layouts: 3.73 us -> 0.01 us
    pallas_call x4 -> x5, Pallas kernels: 31.8 us -> 31.7 us  [the longest x1 12.2 us: combine(): pl.pallas_call(combine_kernel, in_specs=[VMEM, HBM], out_specs=[HBM, HBM]...]
  transfers between devices with their start and end apart: 1 -> 2, of which waited for: 1 -> 2; matrix products, arithmetic and copies ran while one was open for 0% -> 0% of each run, Pallas kernels for 10% -> 17%
where the time goes in v2:
time: 77 us; the launch traced here: 76.6 us
  Pallas kernels  31.7 us (41%)
  starting transfers between devices  24.7 us (32%)
  waiting for transfers between devices  19.5 us (25%)
    all_to_all x1, waiting for transfers between devices, local(): lax.all_to_all(outgoing, DP, split_axis=0, concat_axis=0, tiled=True)  18.9 us
    all_to_all x1, starting transfers between devices, local(): lax.all_to_all(outgoing, DP, split_axis=0, concat_axis=0, tiled=True)  17.1 us
    pallas_call x1, Pallas kernels, combine(): pl.pallas_call(combine_kernel, in_specs=[VMEM, HBM], out_specs=[HBM, HBM]...  12.2 us
    pallas_call x1, Pallas kernels, remain(): pl.pallas_call(functools.partial(remain_kernel, width // LANES), grid=(st...  8.57 us
    all_to_all x1, starting transfers between devices, local(): lax.all_to_all(energy, TENSOR, split_axis=0, concat_axis=0, tiled=True)  7.54 us
    pallas_call x1, Pallas kernels, pick(): pl.pallas_call(functools.partial(pick_kernel, steps), in_specs=[HBM] * 5,...  5.71 us
    pallas_call x1, Pallas kernels, decode(): pl.pallas_call(functools.partial(decode_kernel, steps), in_specs=[HBM, VM...  4.13 us
  transfers between devices with their start and end apart: 2, of which 2 were waited for; matrix products, arithmetic and copies ran while one was open for 0% of the time, Pallas kernels for 17%

profile of v2, /device:TPU:1, one launch (start us, length us, event | category | flops | bytes accessed | tf_op | source)
XLA Modules:
  0.0 76.6 jit_solution(9465542558177229964)
XLA Ops:
  0.6 5.7 %pick.1 = (bf16[64,64,128]{2,1,0:T(8,128)(2,1)}, f32[64,128]{1,0:T(8,128)S(1)}) custom-call(bf16[64,8192]{1,0:T(8,128)(2,1)} %bitcast.6, bf16[64,8192]{1,0:T(8,128)(2,1)} %bitcast.8, s32[32,128]{1,0:T(8,128)} %bitcast.11, bf16[2,256,256]{2,1,0:T(8,128)(2,1)} %constant.8.clone.right_in.right_ref, bf16[64,192]{1,0:T(8,128)(2,1)} %constant.9.clone.left_in.left_ref), custom_call_target="tpu_custom_call" | custom-call | tf_op jit(solution)/shard_map/pick/pallas_call | solution.py:178
  6.3 0.0 copy-start
  6.4 17.1 %all-to-all-start = ((bf16[64,64,128]{2,1,0:T(8,128)(2,1)}), bf16[64,64,128]{2,1,0:T(8,128)(2,1)S(1)}, u32[]{:S(2)}, u32[]{:S(2)}) async-start(bf16[64,64,128]{2,1,0:T(8,128)(2,1)} %get-tuple-element.7), calls=%async_computation | async-start | bytes 2097152 | tf_op jit(solution)/shard_map/all_to_all | solution.py:379
  23.5 0.0 copy-done
  23.5 8.6 %remain.1.after_ref = bf16[64,8192]{1,0:T(8,128)(2,1)} custom-call(bf16[64,8192]{1,0:T(8,128)(2,1)} %bitcast.7, bf16[64,8192]{1,0:T(8,128)(2,1)} %bitcast.9, f32[64,128]{1,0:T(8,128)} %copy-done, bf16[2,256,256]{2,1,0:T(8,128)(2,1)} %constant.8.clone.right_in.right_ref, bf16[64,192]{1,0:T(8,128)(2,1)} %constant.9.clone.left_in.left_ref, ...), custom_call_target="tpu_custom_call" | custom-call | flops 5000000000 | bytes 3145728 | tf_op jit(solution)/shard_map/remain/pallas_call | solution.py:219
  32.1 0.0 copy-start.1
  32.1 0.0 copy-start.2
  32.1 18.9 %all-to-all-done.in_ref = bf16[64,64,128]{2,1,0:T(8,128)(2,1)S(1)} async-done(((bf16[64,64,128]{2,1,0:T(8,128)(2,1)}), bf16[64,64,128]{2,1,0:T(8,128)(2,1)S(1)}, u32[]{:S(2)}, u32[]{:S(2)}) %all-to-all-start) | async-done | bytes 1048608 | tf_op jit(solution)/shard_map/all_to_all | solution.py:379
  51.0 12.2 %combine.1 = (f32[2048,256]{1,0:T(8,128)}, f32[8,8,128]{2,1,0:T(8,128)}) custom-call(bf16[64,64,128]{2,1,0:T(8,128)(2,1)S(1)} %all-to-all-done.in_ref, bf16[64,8192]{1,0:T(8,128)(2,1)} %remain.1.after_ref), custom_call_target="tpu_custom_call" | custom-call | tf_op jit(solution)/shard_map/combine/pallas_call | solution.py:293
  63.2 7.5 %all-to-all-start.1 = ((f32[8,8,128]{2,1,0:T(8,128)}), f32[8,8,128]{2,1,0:T(8,128)S(1)}, u32[]{:S(2)}, u32[]{:S(2)}) async-start(f32[8,8,128]{2,1,0:T(8,128)} %get-tuple-element.9), calls=%async_computation.1 | async-start | bytes 65536 | tf_op jit(solution)/shard_map/all_to_all | solution.py:382
  70.7 0.0 copy-done.1
  70.7 0.0 copy-done.2
  70.7 4.1 %decode.1.decoded_ref = f32[64,8192]{1,0:T(8,128)S(1)} custom-call(f32[2048,256]{1,0:T(8,128)} %get-tuple-element.8.sum_in, bf16[2,256,256]{2,1,0:T(8,128)(2,1)S(1)} %copy-done.1, bf16[64,192]{1,0:T(8,128)(2,1)S(1)} %copy-done.2), custom_call_target="tpu_custom_call" | custom-call | flops 2000000000 | bytes 4194304 | tf_op jit(solution)/shard_map/decode/pallas_call | solution.py:323
  74.9 0.6 all-to-all-done.1.energy_ref
  75.4 1.1 %scale.1 = bf16[64,8192]{1,0:T(8,128)(2,1)} custom-call(f32[64,8192]{1,0:T(8,128)S(1)} %decode.1.decoded_ref, f32[8,8,128]{2,1,0:T(8,128)S(1)} %all-to-all-done.1.energy_ref), custom_call_target="tpu_custom_call" | custom-call | tf_op jit(solution)/shard_map/scale/pallas_call | solution.py:351
Async XLA Ops:
  6.3 17.2 %copy-start = (f32[64,128]{1,0:T(8,128)}, f32[64,128]{1,0:T(8,128)S(1)}, u32[]{:S(2)}) copy-start(f32[64,128]{1,0:T(8,128)S(1)} %get-tuple-element.6.rows_ref) | copy-start | bytes 98308
  6.4 44.6 %all-to-all-start = ((bf16[64,64,128]{2,1,0:T(8,128)(2,1)}), bf16[64,64,128]{2,1,0:T(8,128)(2,1)S(1)}, u32[]{:S(2)}, u32[]{:S(2)}) async-start(bf16[64,64,128]{2,1,0:T(8,128)(2,1)} %get-tuple-element.7), calls=%async_computation | async-start | bytes 2097152 | tf_op jit(solution)/shard_map/all_to_all | solution.py:379
  32.1 38.6 %copy-start.1 = (bf16[2,256,256]{2,1,0:T(8,128)(2,1)S(1)}, bf16[2,256,256]{2,1,0:T(8,128)(2,1)}, u32[]{:S(2)}) copy-start(bf16[2,256,256]{2,1,0:T(8,128)(2,1)} %constant.10.clone.back_right_ref.right_ref) | copy-start | bytes 786436
  32.1 38.6 %copy-start.2 = (bf16[64,192]{1,0:T(8,128)(2,1)S(1)}, bf16[64,192]{1,0:T(8,128)(2,1)}, u32[]{:S(2)}) copy-start(bf16[64,192]{1,0:T(8,128)(2,1)} %constant.11.clone.back_left_ref.left_ref) | copy-start | bytes 73732
  63.2 12.3 %all-to-all-start.1 = ((f32[8,8,128]{2,1,0:T(8,128)}), f32[8,8,128]{2,1,0:T(8,128)S(1)}, u32[]{:S(2)}, u32[]{:S(2)}) async-start(f32[8,8,128]{2,1,0:T(8,128)} %get-tuple-element.9), calls=%async_computation.1 | async-start | bytes 65536 | tf_op jit(solution)/shard_map/all_to_all | solution.py:382

commit v3 on v2

v3 whole, which is shorter than its diff:
```python
import functools

import jax
import jax.numpy as jnp
import numpy as np
from jax import lax
from jax.experimental import pallas as pl
from jax.experimental.pallas import tpu as pltpu
from jax.sharding import Mesh
from jax.sharding import PartitionSpec as P

BLOCK = 64
LANES = 256
QUAD = 4
TENSOR = ("tensor_0", "tensor_1")
DP = ("dp_0", "dp_1")
EVERY = DP + TENSOR

EPSILON = 1e-06
DECAY = 0.999
F32 = jnp.float32
BF16 = jnp.bfloat16


def dct_basis():
    frequency = np.arange(BLOCK, dtype=np.float64)[:, None]
    position = np.arange(BLOCK, dtype=np.float64)[None, :]
    waves = np.cos(np.pi * (2.0 * position + 1.0) * frequency / (2.0 * BLOCK))
    return (waves * np.where(frequency == 0.0, np.sqrt(1.0 / BLOCK), np.sqrt(2.0 / BLOCK))).astype(np.float32)


def constant_halves(x):
    high = x.astype(BF16)
    return high, (x - high.astype(np.float32)).astype(BF16)


def from_left(cosines):
    high, low = constant_halves(cosines)
    return jnp.asarray(np.concatenate([high, high, low], axis=1))


def from_right(cosines):
    return jnp.asarray(np.stack(constant_halves(np.kron(np.eye(QUAD, dtype=np.float32), cosines))))


def halves(x):
    high = x.astype(BF16)
    return high, (x - high.astype(F32)).astype(BF16)


def dot(a, b):
    return lax.dot_general(a, b, (((1,), (0,)), ((), ())), preferred_element_type=F32)


def dot_t(a, b):
    return lax.dot_general(a, b, (((1,), (1,)), ((), ())), preferred_element_type=F32)


def times_right(tiles, right_ref):
    high, low = halves(tiles)
    return dot(high, right_ref[0]) + dot(low, right_ref[0]) + dot(high, right_ref[1])


def times_left(left_ref, tile):
    high, low = halves(tile)
    return dot(left_ref[...], jnp.concatenate([high, low, high], axis=0))


def iota(shape, dim, kind=F32):
    return lax.broadcasted_iota(jnp.int32, shape, dim).astype(kind)


def hot(hit):
    return jnp.where(hit, jnp.ones(hit.shape, BF16), jnp.zeros(hit.shape, BF16))


def one_hot(hit):
    return jnp.where(hit, 1.0, 0.0).astype(BF16)


def col_hits(rows_ref, group, groups):
    col = rows_ref[pl.ds(groups + group, 1), :].astype(BF16)
    return hot(iota((LANES, col.shape[1]), 0).astype(BF16) == col)


def row_levels(rows_ref, group):
    row = rows_ref[pl.ds(group, 1), :]
    return row, iota((BLOCK, row.shape[1]), 0)


def spectra(gradient_ref, momentum_ref, right_ref, left_ref, tiles, first=0):
    cuts = [slice((first + t) * LANES, (first + t + 1) * LANES) for t in range(tiles)]
    renewed = [DECAY * momentum_ref[:, c].astype(F32) + gradient_ref[:, c].astype(F32) for c in cuts]
    half = times_right(jnp.concatenate(renewed, axis=0), right_ref)
    return renewed, [times_left(left_ref, half[t * BLOCK : (t + 1) * BLOCK]) for t in range(tiles)]


def lay_rows(index, rows_ref):
    selected, spans = index.shape
    groups, count = spans // QUAD, selected * QUAD
    copies = one_hot(iota((selected, count), 0, jnp.int32) == iota((selected, count), 1, jnp.int32) % selected)
    keep = iota((spans, count), 0, jnp.int32) % QUAD == iota((spans, count), 1, jnp.int32) // selected
    collect = one_hot(iota((groups, spans), 0, jnp.int32) == iota((groups, spans), 1, jnp.int32) // QUAD)
    span_start = (iota((1, count), 1, jnp.int32) // selected * BLOCK).astype(F32)
    for part, table in enumerate((index // BLOCK, index % BLOCK)):
        turned = jnp.transpose(table.astype(F32)).astype(BF16)
        laid = dot(collect, jnp.where(keep, dot(turned, copies), 0.0).astype(BF16))
        rows_ref[part * groups : (part + 1) * groups, :] = laid + span_start if part else laid


def pick_kernel(
    steps, gradient_in, momentum_in, index_in, right_in, left_in, out_ref, rows_ref,
    gradient_ref, momentum_ref, index_ref, right_ref, left_ref, payload_ref, loaded, sent
):
    width = gradient_ref.shape[1] // steps
    tiles = width // LANES
    tables = [
        pltpu.make_async_copy(source, target, loaded.at[2 * steps + k])
        for k, (source, target) in enumerate(((index_in, index_ref), (right_in, right_ref), (left_in, left_ref)))
    ]
    loads = []
    for step in range(steps):
        part = (slice(None), pl.ds(step * width, width))
        loads.append(
            [
                pltpu.make_async_copy(source.at[part], target.at[part], loaded.at[2 * step + k])
                for k, (source, target) in enumerate(((gradient_in, gradient_ref), (momentum_in, momentum_ref)))
            ]
        )
    for group in [tables, *loads]:
        for load in group:
            load.start()
    tables[0].wait()
    index = index_ref[...]
    groups = index.shape[1] // QUAD
    lay_rows(index, rows_ref)
    rows = []
    for load in tables[1:]:
        load.wait()
    for step in range(steps):
        for load in loads[step]:
            load.wait()
        _, spectrum = spectra(gradient_ref, momentum_ref, right_ref, left_ref, tiles, step * tiles)
        for t in range(tiles):
            by_col = dot(spectrum[t].astype(BF16), col_hits(rows_ref, step * tiles + t, groups))
            row, levels = row_levels(rows_ref, step * tiles + t)
            rows.append(jnp.sum(jnp.where(levels == row, by_col, 0.0), axis=0, keepdims=True))
    row = rows_ref[:groups, :].astype(jnp.int32)
    scale = jnp.ones(row.shape, F32)
    for bit in range(6):
        scale = jnp.where((row >> bit) & 1 == 1, scale * float(2 ** (2**bit)), scale)
    col = rows_ref[groups:, :].astype(jnp.int32) % BLOCK
    coded = (BLOCK + col).astype(F32) * scale
    picked = jnp.concatenate(rows, axis=0)
    shares = payload_ref.shape[0]
    own = groups // shares
    for share in range(shares):
        part = slice(share * own, (share + 1) * own)
        payload_ref[share] = jnp.concatenate([picked[part], coded[part]], axis=0).astype(BF16)
    core = lax.axis_index(TENSOR[1])
    for peer in range(out_ref.shape[0]):
        along_first, along_second = peer // shares, peer % shares
        share = along_second + (along_first - along_second) * core
        pltpu.make_async_copy(payload_ref.at[share], out_ref.at[peer], sent).start()
    pltpu.make_async_copy(out_ref, out_ref, sent).wait()


VMEM = pl.BlockSpec(memory_space=pltpu.VMEM)
HBM = pl.BlockSpec(memory_space=pltpu.HBM)
LIMIT = pltpu.CompilerParams(vmem_limit_bytes=24 * 2**20)


def whole(shape):
    return pl.BlockSpec(shape, lambda i: (0,) * len(shape))


def pick(gradient, momentum, index, right, left, shares, steps=2):
    selected, spans = index.shape
    groups, count = spans // QUAD, selected * QUAD
    share_shape = (2 * groups // shares, count)
    return pl.pallas_call(
        functools.partial(pick_kernel, steps),
        in_specs=[HBM] * 5,
        out_specs=[HBM, VMEM],
        out_shape=[pltpu.HBM((shares * shares, *share_shape), BF16), pltpu.VMEM((2 * groups, count), F32)],
        scratch_shapes=[
            pltpu.VMEM(gradient.shape, BF16),
            pltpu.VMEM(momentum.shape, BF16),
            pltpu.VMEM(index.shape, jnp.int32),
            pltpu.VMEM(right.shape, BF16),
            pltpu.VMEM(left.shape, BF16),
            pltpu.VMEM((shares, *share_shape), BF16),
            pltpu.SemaphoreType.DMA((2 * steps + 3,)),
            pltpu.SemaphoreType.DMA,
        ],
        name="pick",
    )(gradient, momentum, index, right, left)


def remain_kernel(tiles, gradient_ref, momentum_ref, rows_ref, right_ref, left_ref, back_right_ref, back_left_ref, out_ref):
    step = pl.program_id(0)
    groups = rows_ref.shape[0] // 2
    renewed, spectrum = spectra(gradient_ref, momentum_ref, right_ref, left_ref, tiles)
    kept = []
    for t in range(tiles):
        row, levels = row_levels(rows_ref, step * tiles + t)
        marker = dot_t(hot(levels.astype(BF16) == row.astype(BF16)), col_hits(rows_ref, step * tiles + t, groups))
        kept.append(spectrum[t] * marker)
    half = times_right(jnp.concatenate(kept, axis=0), back_right_ref)
    for t in range(tiles):
        restored = times_left(back_left_ref, half[t * BLOCK : (t + 1) * BLOCK])
        out_ref[:, t * LANES : (t + 1) * LANES] = (renewed[t] - restored).astype(BF16)


def remain(gradient, momentum, rows, right, left, back_right, back_left, steps=4):
    height, columns = gradient.shape
    width = columns // steps
    slab = pl.BlockSpec((height, width), lambda i: (0, i))
    return pl.pallas_call(
        functools.partial(remain_kernel, width // LANES),
        grid=(steps,),
        in_specs=[slab, slab, VMEM] + [whole(a.shape) for a in (right, left, back_right, back_left)],
        out_specs=slab,
        out_shape=jax.ShapeDtypeStruct((height, columns), BF16),
        name="remain",
        cost_estimate=pl.CostEstimate(flops=5_000_000_000, bytes_accessed=6 * height * columns, transcendentals=0),
    )(gradient, momentum, rows, right, left, back_right, back_left)


def combine_kernel(in_ref, right_ref, left_ref, block_ref, energy_ref, stage_ref, table_ref, sum_ref):
    sources, double, count = in_ref.shape
    groups, selected = double // 2, count // QUAD
    halved = 128 // sources
    rows = selected // halved
    for source in range(sources):
        stage_ref[source * double : (source + 1) * double, :] = in_ref[source].astype(F32)

    def turned(table):
        shifted = [table] + [pltpu.roll(table, count - h * rows, 1) for h in range(1, halved)]
        return jnp.transpose(jnp.concatenate(shifted, axis=0))

    for g in range(groups):
        value = stage_ref[pl.ds(g, sources, stride=double), :]
        code = stage_ref[pl.ds(groups + g, sources, stride=double), :]
        row = jnp.zeros(code.shape, F32)
        for shift in (32, 16, 8, 4, 2, 1):
            above = code >= BLOCK * 2.0**shift
            code = jnp.where(above, code * 2.0**-shift, code)
            row = jnp.where(above, row + float(shift), row)
        for k, table in enumerate((value, row, code - float(BLOCK))):
            table_ref[3 * g + k] = turned(table)
    levels = iota((BLOCK, 2 * 128), 0).astype(BF16)
    zero = jnp.zeros(levels.shape, BF16)
    one = jnp.ones(levels.shape, BF16)
    energy = jnp.zeros((8, BLOCK), F32)
    for g in range(groups):
        parts = []
        for q in range(QUAD):
            total = None
            for r in range(0, rows, 2):
                at = q * selected + r
                value, row, col = (
                    jnp.concatenate([table_ref[3 * g + k, at + i : at + i + 1, :] for i in range(2)], axis=1).astype(BF16)
                    for k in range(3)
                )
                by_row = jnp.where(levels == row, jnp.broadcast_to(value, levels.shape), zero)
                term = dot_t(by_row, jnp.where(levels == col, one, zero))
                total = term if total is None else total + term
            square = total * total
            for r in range(0, BLOCK, 8):
                energy = energy + square[r : r + 8]
            parts.append(total)
        sum_ref[g * BLOCK : (g + 1) * BLOCK, :] = jnp.concatenate(parts, axis=1)
    energy = jnp.concatenate([energy, jnp.zeros_like(energy)], axis=1)
    for peer in range(energy_ref.shape[0]):
        energy_ref[peer] = energy
    half = times_right(sum_ref[...], right_ref)
    for g in range(groups):
        tile = times_left(left_ref, half[g * BLOCK : (g + 1) * BLOCK]).astype(BF16)
        for k in range(LANES // 128):
            at = (g * (LANES // 128) + k) * BLOCK
            block_ref[at : at + BLOCK, :] = tile[:, k * 128 : (k + 1) * 128]


def combine(received, right, left, rows):
    sources, double, count = received.shape
    height = double // 2 * BLOCK
    return pl.pallas_call(
        combine_kernel,
        in_specs=[VMEM] * 3,
        out_specs=[VMEM, VMEM],
        out_shape=[
            jax.ShapeDtypeStruct((height * LANES // 128, 128), BF16),
            jax.ShapeDtypeStruct((rows, 8, 128), F32),
        ],
        scratch_shapes=[
            pltpu.VMEM((sources * double, count), F32),
            pltpu.VMEM((3 * double // 2, 128, 128), F32),
            pltpu.VMEM((height, LANES), F32),
        ],
        compiler_params=LIMIT,
        name="combine",
    )(received, right, left)


def pack_kernel(block_in, energy_ref, out_ref, block_ref, stamp_ref, loaded, sent):
    height = block_ref.shape[0]
    load = pltpu.make_async_copy(block_in, block_ref, loaded)
    load.start()
    total = jnp.sum(energy_ref[...], axis=0)
    total = jnp.sum(jnp.sum(total, axis=0, keepdims=True), axis=1, keepdims=True)
    pieces = []
    for _ in range(3):
        pieces.append(total.astype(BF16).astype(F32))
        total = total - pieces[-1]
    at = iota(stamp_ref.shape, 0, jnp.int32)
    stamp = jnp.zeros(stamp_ref.shape, F32)
    for k, piece in enumerate(pieces):
        stamp = jnp.where(at == k, piece, stamp)
    stamp_ref[...] = stamp.astype(BF16)
    load.wait()
    for peer in range(out_ref.shape[0]):
        pltpu.make_async_copy(block_ref, out_ref.at[peer, pl.ds(0, height)], sent).start()
        pltpu.make_async_copy(stamp_ref, out_ref.at[peer, pl.ds(height, 8)], sent).start()
    pltpu.make_async_copy(out_ref, out_ref, sent).wait()


def pack(block, energies, peers):
    height, lanes = block.shape
    return pl.pallas_call(
        pack_kernel,
        in_specs=[HBM, VMEM],
        out_specs=HBM,
        out_shape=pltpu.HBM((peers, height + 8, lanes), BF16),
        scratch_shapes=[pltpu.VMEM(block.shape, BF16), pltpu.VMEM((8, lanes), BF16)] + [pltpu.SemaphoreType.DMA] * 2,
        compiler_params=LIMIT,
        name="pack",
    )(block, energies)


def scale_kernel(count, in_ref, after_ref, out_ref, scaled_ref, stored):
    shares, height, lanes = in_ref.shape
    height = height - 8
    total = jnp.zeros((1, 1), F32)
    for share in range(shares):
        stamp = in_ref[share, height:, :].astype(F32)
        total = total + jnp.sum(stamp[:, :1], axis=0, keepdims=True)
    factor = lax.rsqrt(total * (1.0 / count) + EPSILON)
    stores = []
    for share in range(shares):
        pieces = height // BLOCK
        for piece in range(pieces):
            tile = in_ref[share, piece * BLOCK : (piece + 1) * BLOCK, :].astype(F32)
            at = (share * pieces + piece) * lanes
            scaled_ref[:, at : at + lanes] = (tile * factor).astype(BF16)
        if share % 2:
            part = (slice(None), pl.ds((share - 1) * pieces * lanes, 2 * pieces * lanes))
            stores.append(pltpu.make_async_copy(scaled_ref.at[part], out_ref.at[part], stored.at[share // 2]))
            stores[-1].start()
    for store in stores:
        store.wait()


def scale(gathered, after, count):
    shares, height, lanes = gathered.shape
    shape = (BLOCK, shares * (height - 8) // BLOCK * lanes)
    return pl.pallas_call(
        functools.partial(scale_kernel, count),
        in_specs=[VMEM, HBM],
        out_specs=HBM,
        out_shape=pltpu.HBM(shape, BF16),
        scratch_shapes=[pltpu.VMEM(shape, BF16), pltpu.SemaphoreType.DMA((shares // 2,))],
        compiler_params=LIMIT,
        name="scale",
    )(gathered, after)


def places():
    sizes = [lax.axis_size(axis) for axis in EVERY]
    return np.arange(np.prod(sizes)).reshape(sizes)


def gather_lines():
    place = places()
    groups = []
    for chip in range(place.shape[2]):
        groups.extend(place[:, :, chip, 0].tolist())
        groups.extend(place[:, :, chip, 1].T.tolist())
    return groups


def share_holders():
    place = places()
    return [
        [*place[first, second, :, 0].tolist(), *place[second, first, :, 1].tolist()]
        for first in range(place.shape[0])
        for second in range(place.shape[1])
    ]


def exchange(copies, groups):
    return lax.all_to_all(copies, EVERY, split_axis=0, concat_axis=0, axis_index_groups=groups, tiled=True)


def in_vmem(x):
    return pltpu.with_memory_space_constraint(x, pltpu.VMEM)


def in_hbm(x):
    return pltpu.with_memory_space_constraint(x, pltpu.HBM)


def local(gradient, momentum, indices):
    gradient, momentum = in_hbm(gradient[0]), in_hbm(momentum[0])
    height, columns = gradient.shape
    cosines = dct_basis()
    right, left = from_right(cosines.T), from_left(cosines)
    back_right, back_left = from_right(cosines), from_left(cosines.T)
    index = indices.reshape(indices.shape[-2:]).T
    shares, rows = lax.axis_size(DP[0]), lax.axis_size(TENSOR)
    outgoing, index_rows = pick(gradient, momentum, in_hbm(index), in_hbm(right), in_hbm(left), shares)
    received = lax.all_to_all(outgoing, DP, split_axis=0, concat_axis=0, tiled=True)
    block, energy = combine(in_vmem(received), in_vmem(back_right), in_vmem(back_left), rows)
    energies = exchange(energy, share_holders())
    gathered = exchange(pack(in_hbm(block), in_vmem(energies), shares), gather_lines())
    new_momentum = remain(gradient, momentum, index_rows, right, left, back_right, back_left)
    update = scale(in_vmem(gathered), in_hbm(new_momentum), height * columns * rows)
    return (new_momentum[None], update)


def solution(mesh):
    split = Mesh(mesh.devices.reshape(8, 8, 4, 2), ("dp_0", "dp_1", "tensor_0", "tensor_1"))
    placed = (P(DP, TENSOR, None), P(DP, TENSOR, None), P(DP, TENSOR, None, None))
    return jax.shard_map(
        local,
        mesh=split,
        in_specs=placed,
        out_specs=(P(DP, TENSOR, None), P(TENSOR, None)),
        check_vma=False,
    )
```

time: 77 us -> 83.4 us (1.083)
  the two profiles are of different devices: /device:TPU:1 before, /device:TPU:2 now
where the time goes in v3:
time: 83.4 us; the launch traced here: 83.1 us
  blocking collectives  37.9 us (45%)
  Pallas kernels  18.9 us (23%)
  starting transfers between devices  14.5 us (17%)
  waiting for transfers between devices  10.6 us (13%)
    all_to_all x1, blocking collectives, local(): lax.all_to_all(outgoing, DP, split_axis=0, concat_axis=0, tiled=True)  29.3 us
    all_to_all x1, starting transfers between devices, exchange(): lax.all_to_all(copies, EVERY, split_axis=0, concat_axis=0, axis_index_gro...  14.5 us
    all_to_all x1, waiting for transfers between devices, exchange(): lax.all_to_all(copies, EVERY, split_axis=0, concat_axis=0, axis_index_gro...  10.6 us
    all_to_all x1, blocking collectives, exchange(): lax.all_to_all(copies, EVERY, split_axis=0, concat_axis=0, axis_index_gro...  8.56 us
    pallas_call x1, Pallas kernels, remain(): pl.pallas_call(functools.partial(remain_kernel, width // LANES), grid=(st...  8.55 us
    pallas_call x1, Pallas kernels, pick(): pl.pallas_call(functools.partial(pick_kernel, steps), in_specs=[HBM] * 5,...  5.3 us
    pallas_call x1, Pallas kernels, combine(): pl.pallas_call(combine_kernel, in_specs=[VMEM] * 3, out_specs=[VMEM, VMEM...  1.97 us
    pallas_call x1, Pallas kernels, pack(): pl.pallas_call(pack_kernel, in_specs=[HBM, VMEM], out_specs=HBM, out_shap...  1.89 us
  transfers between devices with their start and end apart: 1, of which 1 were waited for; matrix products, arithmetic and copies ran while one was open for 0% of the time, Pallas kernels for 10%

profile of v3, /device:TPU:2, one launch (start us, length us, event | category | flops | bytes accessed | tf_op | source)
XLA Modules:
  0.0 83.1 jit_solution(15187342954560430682)
XLA Ops:
  0.6 0.0 copy-start
  0.6 0.0 copy-start.2
  0.7 5.3 %pick.1 = (bf16[64,8,128]{2,1,0:T(8,128)(2,1)}, f32[64,128]{1,0:T(8,128)S(1)}) custom-call(bf16[64,8192]{1,0:T(8,128)(2,1)} %bitcast.7, bf16[64,8192]{1,0:T(8,128)(2,1)} %bitcast.9, s32[32,128]{1,0:T(8,128)} %bitcast.11, bf16[2,256,256]{2,1,0:T(8,128)(2,1)} %constant.8.clone.right_in.right_ref, bf16[64,192]{1,0:T(8,128)(2,1)} %constant.9.clone.left_in.left_ref), custom_call_target="tpu_custom_call" | custom-call | tf_op jit(solution)/shard_map/pick/pallas_call | solution.py:181
  6.0 0.0 copy-start.3
  6.0 29.3 %all_to_all.15.in_ref = bf16[64,8,128]{2,1,0:T(8,128)(2,1)S(1)} all-to-all(bf16[64,8,128]{2,1,0:T(8,128)(2,1)} %get-tuple-element.7), channel_id=1, replica_groups=mesh['dp_0'=8,'dp_1'=8,'tensor_0'=4,'tensor_1'=2] {'dp_0','dp_1'}, dimensions={0} | all-to-all | bytes 262144 | tf_op jit(solution)/shard_map/all_to_all | solution.py:422
  35.3 0.0 copy-done
  35.3 0.0 copy-done.2
  35.3 2.0 %combine.1 = (bf16[512,128]{1,0:T(8,128)(2,1)S(1)}, f32[8,8,128]{2,1,0:T(8,128)S(1)}) custom-call(bf16[64,8,128]{2,1,0:T(8,128)(2,1)S(1)} %all_to_all.15.in_ref, bf16[2,256,256]{2,1,0:T(8,128)(2,1)S(1)} %copy-done, bf16[64,192]{1,0:T(8,128)(2,1)S(1)} %copy-done.2), custom_call_target="tpu_custom_call" | custom-call | tf_op jit(solution)/shard_map/combine/pallas_call | solution.py:288
  37.3 0.0 copy-start.1
  37.3 0.6 copy-done.1
  37.9 8.6 %all_to_all.16.energy_ref = f32[8,8,128]{2,1,0:T(8,128)S(1)} all-to-all(f32[8,8,128]{2,1,0:T(8,128)S(1)} %get-tuple-element.9), channel_id=1, replica_groups={{0,2,4,6,1,3,5,7},{8,10,12,14,65,67,69,71},{16,18,20,22,129,131,133,135..., dimensions={0} | all-to-all | bytes 65536 | tf_op jit(solution)/shard_map/all_to_all | solution.py:402
  46.5 1.9 %pack.1 = bf16[8,520,128]{2,1,0:T(8,128)(2,1)} custom-call(bf16[512,128]{1,0:T(8,128)(2,1)} %copy-done.1, f32[8,8,128]{2,1,0:T(8,128)S(1)} %all_to_all.16.energy_ref), custom_call_target="tpu_custom_call" | custom-call | tf_op jit(solution)/shard_map/pack/pallas_call | solution.py:330
  48.4 0.0 copy-done.3
  48.4 14.5 %all-to-all-start.2 = ((bf16[8,520,128]{2,1,0:T(8,128)(2,1)}), bf16[8,520,128]{2,1,0:T(8,128)(2,1)S(1)}, u32[]{:S(2)}, u32[]{:S(2)}) async-start(bf16[8,520,128]{2,1,0:T(8,128)(2,1)} %pack.1), calls=%async_computation.2 | async-start | bytes 2129920 | tf_op jit(solution)/shard_map/all_to_all | solution.py:402
  62.9 8.6 %remain.1.after_ref = bf16[64,8192]{1,0:T(8,128)(2,1)} custom-call(bf16[64,8192]{1,0:T(8,128)(2,1)} %bitcast.8, bf16[64,8192]{1,0:T(8,128)(2,1)} %bitcast.10, f32[64,128]{1,0:T(8,128)} %copy-done.3, bf16[2,256,256]{2,1,0:T(8,128)(2,1)} %constant.8.clone.right_in.right_ref, bf16[64,192]{1,0:T(8,128)(2,1)} %constant.9.clone.left_in.left_ref, ...), custom_call_target="tpu_custom_call" | custom-call | flops 5000000000 | bytes 3145728 | tf_op jit(solution)/shard_map/remain/pallas_call | solution.py:219
  71.4 10.6 %all-to-all-done.2.in_ref = bf16[8,520,128]{2,1,0:T(8,128)(2,1)S(1)} async-done(((bf16[8,520,128]{2,1,0:T(8,128)(2,1)}), bf16[8,520,128]{2,1,0:T(8,128)(2,1)S(1)}, u32[]{:S(2)}, u32[]{:S(2)}) %all-to-all-start.2) | async-done | bytes 1064992 | tf_op jit(solution)/shard_map/all_to_all | solution.py:402
  82.0 1.1 %scale.1 = bf16[64,8192]{1,0:T(8,128)(2,1)} custom-call(bf16[8,520,128]{2,1,0:T(8,128)(2,1)S(1)} %all-to-all-done.2.in_ref, bf16[64,8192]{1,0:T(8,128)(2,1)} %remain.1.after_ref), custom_call_target="tpu_custom_call" | custom-call | tf_op jit(solution)/shard_map/scale/pallas_call | solution.py:367
Async XLA Ops:
  0.6 34.7 %copy-start = (bf16[2,256,256]{2,1,0:T(8,128)(2,1)S(1)}, bf16[2,256,256]{2,1,0:T(8,128)(2,1)}, u32[]{:S(2)}) copy-start(bf16[2,256,256]{2,1,0:T(8,128)(2,1)} %constant.10.clone.back_right_ref.right_ref) | copy-start | bytes 786436
  0.6 34.6 %copy-start.2 = (bf16[64,192]{1,0:T(8,128)(2,1)S(1)}, bf16[64,192]{1,0:T(8,128)(2,1)}, u32[]{:S(2)}) copy-start(bf16[64,192]{1,0:T(8,128)(2,1)} %constant.11.clone.back_left_ref.left_ref) | copy-start | bytes 73732
  6.0 42.4 %copy-start.3 = (f32[64,128]{1,0:T(8,128)}, f32[64,128]{1,0:T(8,128)S(1)}, u32[]{:S(2)}) copy-start(f32[64,128]{1,0:T(8,128)S(1)} %get-tuple-element.6.rows_ref) | copy-start | bytes 98308
  37.3 0.7 copy-start.1
  48.4 33.6 %all-to-all-start.2 = ((bf16[8,520,128]{2,1,0:T(8,128)(2,1)}), bf16[8,520,128]{2,1,0:T(8,128)(2,1)S(1)}, u32[]{:S(2)}, u32[]{:S(2)}) async-start(bf16[8,520,128]{2,1,0:T(8,128)(2,1)} %pack.1), calls=%async_computation.2 | async-start | bytes 2129920 | tf_op jit(solution)/shard_map/all_to_all | solution.py:402

commit v4 on v3

--- a/solution.py
+++ b/solution.py
@@ -227,7 +227,7 @@
     )(gradient, momentum, rows, right, left, back_right, back_left)
 
 
-def combine_kernel(in_ref, right_ref, left_ref, block_ref, energy_ref, stage_ref, table_ref, sum_ref):
+def combine_kernel(in_ref, right_ref, left_ref, out_ref, stage_ref, table_ref, sum_ref, block_ref, stamp_ref, sent):
     sources, double, count = in_ref.shape
     groups, selected = double // 2, count // QUAD
     halved = 128 // sources
@@ -271,80 +271,77 @@
                 energy = energy + square[r : r + 8]
             parts.append(total)
         sum_ref[g * BLOCK : (g + 1) * BLOCK, :] = jnp.concatenate(parts, axis=1)
-    energy = jnp.concatenate([energy, jnp.zeros_like(energy)], axis=1)
-    for peer in range(energy_ref.shape[0]):
-        energy_ref[peer] = energy
     half = times_right(sum_ref[...], right_ref)
     for g in range(groups):
         tile = times_left(left_ref, half[g * BLOCK : (g + 1) * BLOCK]).astype(BF16)
         for k in range(LANES // 128):
             at = (g * (LANES // 128) + k) * BLOCK
             block_ref[at : at + BLOCK, :] = tile[:, k * 128 : (k + 1) * 128]
-
-
-def combine(received, right, left, rows):
+    height = block_ref.shape[0]
+    for peer in range(out_ref.shape[0]):
+        pltpu.make_async_copy(block_ref, out_ref.at[peer, pl.ds(0, height)], sent).start()
+    total = jnp.sum(jnp.sum(energy, axis=0, keepdims=True), axis=1, keepdims=True)
+    at = iota(stamp_ref.shape, 0, jnp.int32)
+    stamp = jnp.zeros(stamp_ref.shape, F32)
+    for k in range(3):
+        piece = total.astype(BF16).astype(F32)
+        stamp = jnp.where(at == k, piece, stamp)
+        total = total - piece
+    stamp_ref[...] = stamp.astype(BF16)
+    for peer in range(out_ref.shape[0]):
+        pltpu.make_async_copy(stamp_ref, out_ref.at[peer, pl.ds(height, 8)], sent).start()
+    pltpu.make_async_copy(out_ref, out_ref, sent).wait()
+
+
+def combine(received, right, left, peers):
     sources, double, count = received.shape
     height = double // 2 * BLOCK
+    block = (height * LANES // 128, 128)
     return pl.pallas_call(
         combine_kernel,
         in_specs=[VMEM] * 3,
-        out_specs=[VMEM, VMEM],
-        out_shape=[
-            jax.ShapeDtypeStruct((height * LANES // 128, 128), BF16),
-            jax.ShapeDtypeStruct((rows, 8, 128), F32),
-        ],
+        out_specs=HBM,
+        out_shape=pltpu.HBM((peers, block[0] + 8, block[1]), BF16),
         scratch_shapes=[
             pltpu.VMEM((sources * double, count), F32),
             pltpu.VMEM((3 * double // 2, 128, 128), F32),
             pltpu.VMEM((height, LANES), F32),
+            pltpu.VMEM(block, BF16),
+            pltpu.VMEM((8, 128), BF16),
+            pltpu.SemaphoreType.DMA,
         ],
         compiler_params=LIMIT,
         name="combine",
     )(received, right, left)
 
 
-def pack_kernel(block_in, energy_ref, out_ref, block_ref, stamp_ref, loaded, sent):
-    height = block_ref.shape[0]
-    load = pltpu.make_async_copy(block_in, block_ref, loaded)
-    load.start()
+def total_kernel(in_ref, after_ref, out_ref):
+    total = jnp.zeros((1, 1), F32)
+    for share in range(in_ref.shape[0]):
+        total = total + jnp.sum(in_ref[share, in_ref.shape[1] - 8 :, :].astype(F32)[:, :1], axis=0, keepdims=True)
+    tile = out_ref.shape[1:]
+    corner = jnp.logical_and(iota(tile, 0, jnp.int32) == 0, iota(tile, 1, jnp.int32) == 0)
+    tile = jnp.where(corner, total, 0.0)
+    for peer in range(out_ref.shape[0]):
+        out_ref[peer] = tile
+
+
+def row_total(gathered, after, rows):
+    return pl.pallas_call(
+        total_kernel,
+        in_specs=[VMEM, HBM],
+        out_specs=VMEM,
+        out_shape=pltpu.VMEM((rows, 8, 128), F32),
+        compiler_params=LIMIT,
+        name="row_total",
+    )(gathered, after)
+
+
+def scale_kernel(count, in_ref, energy_ref, out_ref, scaled_ref, stored):
+    shares, height, lanes = in_ref.shape
+    height = height - 8
     total = jnp.sum(energy_ref[...], axis=0)
     total = jnp.sum(jnp.sum(total, axis=0, keepdims=True), axis=1, keepdims=True)
-    pieces = []
-    for _ in range(3):
-        pieces.append(total.astype(BF16).astype(F32))
-        total = total - pieces[-1]
-    at = iota(stamp_ref.shape, 0, jnp.int32)
-    stamp = jnp.zeros(stamp_ref.shape, F32)
-    for k, piece in enumerate(pieces):
-        stamp = jnp.where(at == k, piece, stamp)
-    stamp_ref[...] = stamp.astype(BF16)
-    load.wait()
-    for peer in range(out_ref.shape[0]):
-        pltpu.make_async_copy(block_ref, out_ref.at[peer, pl.ds(0, height)], sent).start()
-        pltpu.make_async_copy(stamp_ref, out_ref.at[peer, pl.ds(height, 8)], sent).start()
-    pltpu.make_async_copy(out_ref, out_ref, sent).wait()
-
-
-def pack(block, energies, peers):
-    height, lanes = block.shape
-    return pl.pallas_call(
-        pack_kernel,
-        in_specs=[HBM, VMEM],
-        out_specs=HBM,
-        out_shape=pltpu.HBM((peers, height + 8, lanes), BF16),
-        scratch_shapes=[pltpu.VMEM(block.shape, BF16), pltpu.VMEM((8, lanes), BF16)] + [pltpu.SemaphoreType.DMA] * 2,
-        compiler_params=LIMIT,
-        name="pack",
-    )(block, energies)
-
-
-def scale_kernel(count, in_ref, after_ref, out_ref, scaled_ref, stored):
-    shares, height, lanes = in_ref.shape
-    height = height - 8
-    total = jnp.zeros((1, 1), F32)
-    for share in range(shares):
-        stamp = in_ref[share, height:, :].astype(F32)
-        total = total + jnp.sum(stamp[:, :1], axis=0, keepdims=True)
     factor = lax.rsqrt(total * (1.0 / count) + EPSILON)
     stores = []
     for share in range(shares):
@@ -361,18 +358,18 @@
         store.wait()
 
 
-def scale(gathered, after, count):
+def scale(gathered, energies, count):
     shares, height, lanes = gathered.shape
     shape = (BLOCK, shares * (height - 8) // BLOCK * lanes)
     return pl.pallas_call(
         functools.partial(scale_kernel, count),
-        in_specs=[VMEM, HBM],
+        in_specs=[VMEM, VMEM],
         out_specs=HBM,
         out_shape=pltpu.HBM(shape, BF16),
         scratch_shapes=[pltpu.VMEM(shape, BF16), pltpu.SemaphoreType.DMA((shares // 2,))],
         compiler_params=LIMIT,
         name="scale",
-    )(gathered, after)
+    )(gathered, energies)
 
 
 def places():
@@ -387,15 +384,6 @@
         groups.extend(place[:, :, chip, 0].tolist())
         groups.extend(place[:, :, chip, 1].T.tolist())
     return groups
-
-
-def share_holders():
-    place = places()
-    return [
-        [*place[first, second, :, 0].tolist(), *place[second, first, :, 1].tolist()]
-        for first in range(place.shape[0])
-        for second in range(place.shape[1])
-    ]
 
 
 def exchange(copies, groups):
@@ -420,11 +408,12 @@
     shares, rows = lax.axis_size(DP[0]), lax.axis_size(TENSOR)
     outgoing, index_rows = pick(gradient, momentum, in_hbm(index), in_hbm(right), in_hbm(left), shares)
     received = lax.all_to_all(outgoing, DP, split_axis=0, concat_axis=0, tiled=True)
-    block, energy = combine(in_vmem(received), in_vmem(back_right), in_vmem(back_left), rows)
-    energies = exchange(energy, share_holders())
-    gathered = exchange(pack(in_hbm(block), in_vmem(energies), shares), gather_lines())
+    shared = combine(in_vmem(received), in_vmem(back_right), in_vmem(back_left), shares)
     new_momentum = remain(gradient, momentum, index_rows, right, left, back_right, back_left)
-    update = scale(in_vmem(gathered), in_hbm(new_momentum), height * columns * rows)
+    gathered = in_vmem(exchange(shared, gather_lines()))
+    energy = row_total(gathered, in_hbm(new_momentum), rows)
+    energies = lax.all_to_all(energy, TENSOR, split_axis=0, concat_axis=0, tiled=True)
+    update = scale(gathered, in_vmem(energies), height * columns * rows)
     return (new_momentum[None], update)
 
 

time: 83.4 us -> 72.7 us (0.87)
  the two profiles are of different devices: /device:TPU:2 before, /device:TPU:1 now
where the time goes in v4:
time: 72.7 us; the launch traced here: 72.4 us
  blocking collectives  40.4 us (56%)
  Pallas kernels  18.1 us (25%)
  waiting for transfers between devices  9.62 us (13%)
  starting transfers between devices  3.57 us (5%)
    all_to_all x1, blocking collectives, local(): lax.all_to_all(outgoing, DP, split_axis=0, concat_axis=0, tiled=True)  28.7 us
    all_to_all x1, blocking collectives, local(): lax.all_to_all(energy, TENSOR, split_axis=0, concat_axis=0, tiled=True)  11.8 us
    all_to_all x1, waiting for transfers between devices, exchange(): lax.all_to_all(copies, EVERY, split_axis=0, concat_axis=0, axis_index_gro...  9.62 us
    pallas_call x1, Pallas kernels, remain(): pl.pallas_call(functools.partial(remain_kernel, width // LANES), grid=(st...  8.57 us
    pallas_call x1, Pallas kernels, pick(): pl.pallas_call(functools.partial(pick_kernel, steps), in_specs=[HBM] * 5,...  5.3 us
    all_to_all x1, starting transfers between devices, exchange(): lax.all_to_all(copies, EVERY, split_axis=0, concat_axis=0, axis_index_gro...  3.57 us
    pallas_call x1, Pallas kernels, combine(): pl.pallas_call(combine_kernel, in_specs=[VMEM] * 3, out_specs=HBM, out_sh...  2.96 us
  transfers between devices with their start and end apart: 1, of which 1 were waited for; matrix products, arithmetic and copies ran while one was open for 0% of the time, Pallas kernels for 12%

profile of v4, /device:TPU:1, one launch (start us, length us, event | category | flops | bytes accessed | tf_op | source)
XLA Modules:
  0.0 72.4 jit_solution(10530521403410984903)
XLA Ops:
  0.6 0.0 copy-start
  0.6 0.0 copy-start.1
  0.7 5.3 %pick.1 = (bf16[64,8,128]{2,1,0:T(8,128)(2,1)}, f32[64,128]{1,0:T(8,128)S(1)}) custom-call(bf16[64,8192]{1,0:T(8,128)(2,1)} %bitcast.6, bf16[64,8192]{1,0:T(8,128)(2,1)} %bitcast.8, s32[32,128]{1,0:T(8,128)} %bitcast.11, bf16[2,256,256]{2,1,0:T(8,128)(2,1)} %constant.8.clone.right_in.right_ref, bf16[64,192]{1,0:T(8,128)(2,1)} %constant.9.clone.left_in.left_ref), custom_call_target="tpu_custom_call" | custom-call | tf_op jit(solution)/shard_map/pick/pallas_call | solution.py:181
  6.0 0.0 copy-start.2
  6.0 28.7 %all_to_all.15.in_ref = bf16[64,8,128]{2,1,0:T(8,128)(2,1)S(1)} all-to-all(bf16[64,8,128]{2,1,0:T(8,128)(2,1)} %get-tuple-element.5), channel_id=1, replica_groups=mesh['dp_0'=8,'dp_1'=8,'tensor_0'=4,'tensor_1'=2] {'dp_0','dp_1'}, dimensions={0} | all-to-all | bytes 262144 | tf_op jit(solution)/shard_map/all_to_all | solution.py:410
  34.6 0.0 copy-done
  34.7 0.0 copy-done.1
  34.7 3.0 %combine.1 = bf16[8,520,128]{2,1,0:T(8,128)(2,1)} custom-call(bf16[64,8,128]{2,1,0:T(8,128)(2,1)S(1)} %all_to_all.15.in_ref, bf16[2,256,256]{2,1,0:T(8,128)(2,1)S(1)} %copy-done, bf16[64,192]{1,0:T(8,128)(2,1)S(1)} %copy-done.1), custom_call_target="tpu_custom_call" | custom-call | tf_op jit(solution)/shard_map/combine/pallas_call | solution.py:300
  37.6 0.0 copy-done.2
  37.6 3.6 %all-to-all-start.1 = ((bf16[8,520,128]{2,1,0:T(8,128)(2,1)}), bf16[8,520,128]{2,1,0:T(8,128)(2,1)S(1)}, u32[]{:S(2)}, u32[]{:S(2)}) async-start(bf16[8,520,128]{2,1,0:T(8,128)(2,1)} %combine.1), calls=%async_computation.1 | async-start | bytes 2129920 | tf_op jit(solution)/shard_map/all_to_all | solution.py:390
  41.2 8.6 %remain.1.after_ref = bf16[64,8192]{1,0:T(8,128)(2,1)} custom-call(bf16[64,8192]{1,0:T(8,128)(2,1)} %bitcast.7, bf16[64,8192]{1,0:T(8,128)(2,1)} %bitcast.9, f32[64,128]{1,0:T(8,128)} %copy-done.2, bf16[2,256,256]{2,1,0:T(8,128)(2,1)} %constant.8.clone.right_in.right_ref, bf16[64,192]{1,0:T(8,128)(2,1)} %constant.9.clone.left_in.left_ref, ...), custom_call_target="tpu_custom_call" | custom-call | flops 5000000000 | bytes 3145728 | tf_op jit(solution)/shard_map/remain/pallas_call | solution.py:219
  49.8 9.6 %all-to-all-done.1.in_ref = bf16[8,520,128]{2,1,0:T(8,128)(2,1)S(1)} async-done(((bf16[8,520,128]{2,1,0:T(8,128)(2,1)}), bf16[8,520,128]{2,1,0:T(8,128)(2,1)S(1)}, u32[]{:S(2)}, u32[]{:S(2)}) %all-to-all-start.1) | async-done | bytes 1064992 | tf_op jit(solution)/shard_map/all_to_all | solution.py:390
  59.4 0.1 row_total.1
  59.5 11.8 %all_to_all.16.energy_ref = f32[8,8,128]{2,1,0:T(8,128)S(1)} all-to-all(f32[8,8,128]{2,1,0:T(8,128)S(1)} %row_total.1), channel_id=1, replica_groups=mesh['dp_0'=8,'dp_1'=8,'tensor_0'=4,'tensor_1'=2] {'tensor_0','tensor_1'}, dimensions={0} | all-to-all | bytes 65536 | tf_op jit(solution)/shard_map/all_to_all | solution.py:415
  71.3 1.1 %scale.1 = bf16[64,8192]{1,0:T(8,128)(2,1)} custom-call(bf16[8,520,128]{2,1,0:T(8,128)(2,1)S(1)} %all-to-all-done.1.in_ref, f32[8,8,128]{2,1,0:T(8,128)S(1)} %all_to_all.16.energy_ref), custom_call_target="tpu_custom_call" | custom-call | tf_op jit(solution)/shard_map/scale/pallas_call | solution.py:364
Async XLA Ops:
  0.6 34.0 %copy-start = (bf16[2,256,256]{2,1,0:T(8,128)(2,1)S(1)}, bf16[2,256,256]{2,1,0:T(8,128)(2,1)}, u32[]{:S(2)}) copy-start(bf16[2,256,256]{2,1,0:T(8,128)(2,1)} %constant.10.clone.back_right_ref.right_ref) | copy-start | bytes 786436
  0.6 34.0 %copy-start.1 = (bf16[64,192]{1,0:T(8,128)(2,1)S(1)}, bf16[64,192]{1,0:T(8,128)(2,1)}, u32[]{:S(2)}) copy-start(bf16[64,192]{1,0:T(8,128)(2,1)} %constant.11.clone.back_left_ref.left_ref) | copy-start | bytes 73732
  6.0 31.7 %copy-start.2 = (f32[64,128]{1,0:T(8,128)}, f32[64,128]{1,0:T(8,128)S(1)}, u32[]{:S(2)}) copy-start(f32[64,128]{1,0:T(8,128)S(1)} %get-tuple-element.4.rows_ref) | copy-start | bytes 98308
  37.6 21.8 %all-to-all-start.1 = ((bf16[8,520,128]{2,1,0:T(8,128)(2,1)}), bf16[8,520,128]{2,1,0:T(8,128)(2,1)S(1)}, u32[]{:S(2)}, u32[]{:S(2)}) async-start(bf16[8,520,128]{2,1,0:T(8,128)(2,1)} %combine.1), calls=%async_computation.1 | async-start | bytes 2129920 | tf_op jit(solution)/shard_map/all_to_all | solution.py:390

commit v5 on v4

--- a/solution.py
+++ b/solution.py
@@ -12,6 +12,7 @@
 BLOCK = 64
 LANES = 256
 QUAD = 4
+SHARES = 2
 TENSOR = ("tensor_0", "tensor_1")
 DP = ("dp_0", "dp_1")
 EVERY = DP + TENSOR
@@ -112,15 +113,14 @@
     steps, gradient_in, momentum_in, index_in, right_in, left_in, out_ref, rows_ref,
     gradient_ref, momentum_ref, index_ref, right_ref, left_ref, payload_ref, loaded, sent
 ):
-    width = gradient_ref.shape[1] // steps
-    tiles = width // LANES
+    starts = np.cumsum([0, *steps])
     tables = [
-        pltpu.make_async_copy(source, target, loaded.at[2 * steps + k])
+        pltpu.make_async_copy(source, target, loaded.at[2 * len(steps) + k])
         for k, (source, target) in enumerate(((index_in, index_ref), (right_in, right_ref), (left_in, left_ref)))
     ]
     loads = []
-    for step in range(steps):
-        part = (slice(None), pl.ds(step * width, width))
+    for step, tiles in enumerate(steps):
+        part = (slice(None), pl.ds(int(starts[step]) * LANES, tiles * LANES))
         loads.append(
             [
                 pltpu.make_async_copy(source.at[part], target.at[part], loaded.at[2 * step + k])
@@ -137,13 +137,14 @@
     rows = []
     for load in tables[1:]:
         load.wait()
-    for step in range(steps):
+    for step, tiles in enumerate(steps):
         for load in loads[step]:
             load.wait()
-        _, spectrum = spectra(gradient_ref, momentum_ref, right_ref, left_ref, tiles, step * tiles)
+        first = int(starts[step])
+        _, spectrum = spectra(gradient_ref, momentum_ref, right_ref, left_ref, tiles, first)
         for t in range(tiles):
-            by_col = dot(spectrum[t].astype(BF16), col_hits(rows_ref, step * tiles + t, groups))
-            row, levels = row_levels(rows_ref, step * tiles + t)
+            by_col = dot(spectrum[t].astype(BF16), col_hits(rows_ref, first + t, groups))
+            row, levels = row_levels(rows_ref, first + t)
             rows.append(jnp.sum(jnp.where(levels == row, by_col, 0.0), axis=0, keepdims=True))
     row = rows_ref[:groups, :].astype(jnp.int32)
     scale = jnp.ones(row.shape, F32)
@@ -158,8 +159,9 @@
         part = slice(share * own, (share + 1) * own)
         payload_ref[share] = jnp.concatenate([picked[part], coded[part]], axis=0).astype(BF16)
     core = lax.axis_index(TENSOR[1])
+    line = lax.axis_size(DP[1])
     for peer in range(out_ref.shape[0]):
-        along_first, along_second = peer // shares, peer % shares
+        along_first, along_second = peer // line % shares, peer % line % shares
         share = along_second + (along_first - along_second) * core
         pltpu.make_async_copy(payload_ref.at[share], out_ref.at[peer], sent).start()
     pltpu.make_async_copy(out_ref, out_ref, sent).wait()
@@ -174,7 +176,7 @@
     return pl.BlockSpec(shape, lambda i: (0,) * len(shape))
 
 
-def pick(gradient, momentum, index, right, left, shares, steps=2):
+def pick(gradient, momentum, index, right, left, shares, steps=(8, 24)):
     selected, spans = index.shape
     groups, count = spans // QUAD, selected * QUAD
     share_shape = (2 * groups // shares, count)
@@ -182,7 +184,7 @@
         functools.partial(pick_kernel, steps),
         in_specs=[HBM] * 5,
         out_specs=[HBM, VMEM],
-        out_shape=[pltpu.HBM((shares * shares, *share_shape), BF16), pltpu.VMEM((2 * groups, count), F32)],
+        out_shape=[pltpu.HBM((lax.axis_size(DP), *share_shape), BF16), pltpu.VMEM((2 * groups, count), F32)],
         scratch_shapes=[
             pltpu.VMEM(gradient.shape, BF16),
             pltpu.VMEM(momentum.shape, BF16),
@@ -190,7 +192,7 @@
             pltpu.VMEM(right.shape, BF16),
             pltpu.VMEM(left.shape, BF16),
             pltpu.VMEM((shares, *share_shape), BF16),
-            pltpu.SemaphoreType.DMA((2 * steps + 3,)),
+            pltpu.SemaphoreType.DMA((2 * len(steps) + 3,)),
             pltpu.SemaphoreType.DMA,
         ],
         name="pick",
@@ -227,7 +229,7 @@
     )(gradient, momentum, rows, right, left, back_right, back_left)
 
 
-def combine_kernel(in_ref, right_ref, left_ref, out_ref, stage_ref, table_ref, sum_ref, block_ref, stamp_ref, sent):
+def combine_kernel(in_ref, right_ref, left_ref, after_ref, out_ref, stage_ref, table_ref, sum_ref, block_ref, stamp_ref, sent):
     sources, double, count = in_ref.shape
     groups, selected = double // 2, count // QUAD
     halved = 128 // sources
@@ -293,13 +295,13 @@
     pltpu.make_async_copy(out_ref, out_ref, sent).wait()
 
 
-def combine(received, right, left, peers):
+def combine(received, right, left, after, peers):
     sources, double, count = received.shape
     height = double // 2 * BLOCK
     block = (height * LANES // 128, 128)
     return pl.pallas_call(
         combine_kernel,
-        in_specs=[VMEM] * 3,
+        in_specs=[VMEM] * 3 + [HBM],
         out_specs=HBM,
         out_shape=pltpu.HBM((peers, block[0] + 8, block[1]), BF16),
         scratch_shapes=[
@@ -312,10 +314,10 @@
         ],
         compiler_params=LIMIT,
         name="combine",
-    )(received, right, left)
-
-
-def total_kernel(in_ref, after_ref, out_ref):
+    )(received, right, left, after)
+
+
+def total_kernel(in_ref, out_ref):
     total = jnp.zeros((1, 1), F32)
     for share in range(in_ref.shape[0]):
         total = total + jnp.sum(in_ref[share, in_ref.shape[1] - 8 :, :].astype(F32)[:, :1], axis=0, keepdims=True)
@@ -326,15 +328,15 @@
         out_ref[peer] = tile
 
 
-def row_total(gathered, after, rows):
+def row_total(gathered, rows):
     return pl.pallas_call(
         total_kernel,
-        in_specs=[VMEM, HBM],
+        in_specs=[VMEM],
         out_specs=VMEM,
         out_shape=pltpu.VMEM((rows, 8, 128), F32),
         compiler_params=LIMIT,
         name="row_total",
-    )(gathered, after)
+    )(gathered)
 
 
 def scale_kernel(count, in_ref, energy_ref, out_ref, scaled_ref, stored):
@@ -344,15 +346,15 @@
     total = jnp.sum(jnp.sum(total, axis=0, keepdims=True), axis=1, keepdims=True)
     factor = lax.rsqrt(total * (1.0 / count) + EPSILON)
     stores = []
-    for share in range(shares):
-        pieces = height // BLOCK
-        for piece in range(pieces):
-            tile = in_ref[share, piece * BLOCK : (piece + 1) * BLOCK, :].astype(F32)
-            at = (share * pieces + piece) * lanes
-            scaled_ref[:, at : at + lanes] = (tile * factor).astype(BF16)
-        if share % 2:
-            part = (slice(None), pl.ds((share - 1) * pieces * lanes, 2 * pieces * lanes))
-            stores.append(pltpu.make_async_copy(scaled_ref.at[part], out_ref.at[part], stored.at[share // 2]))
+    pieces = height // BLOCK
+    batch = shares * pieces // stored.shape[0]
+    for piece in range(shares * pieces):
+        inside = piece % pieces * BLOCK
+        tile = in_ref[piece // pieces, inside : inside + BLOCK, :].astype(F32)
+        scaled_ref[:, piece * lanes : (piece + 1) * lanes] = (tile * factor).astype(BF16)
+        if (piece + 1) % batch == 0:
+            part = (slice(None), pl.ds((piece + 1 - batch) * lanes, batch * lanes))
+            stores.append(pltpu.make_async_copy(scaled_ref.at[part], out_ref.at[part], stored.at[piece // batch]))
             stores[-1].start()
     for store in stores:
         store.wait()
@@ -366,7 +368,7 @@
         in_specs=[VMEM, VMEM],
         out_specs=HBM,
         out_shape=pltpu.HBM(shape, BF16),
-        scratch_shapes=[pltpu.VMEM(shape, BF16), pltpu.SemaphoreType.DMA((shares // 2,))],
+        scratch_shapes=[pltpu.VMEM(shape, BF16), pltpu.SemaphoreType.DMA((4,))],
         compiler_params=LIMIT,
         name="scale",
     )(gathered, energies)
@@ -377,12 +379,12 @@
     return np.arange(np.prod(sizes)).reshape(sizes)
 
 
-def gather_lines():
+def share_holders(shares):
     place = places()
     groups = []
     for chip in range(place.shape[2]):
-        groups.extend(place[:, :, chip, 0].tolist())
-        groups.extend(place[:, :, chip, 1].T.tolist())
+        groups.extend(place[:, :, chip, 0].reshape(-1, shares).tolist())
+        groups.extend(place[:, :, chip, 1].T.reshape(-1, shares).tolist())
     return groups
 
 
@@ -405,13 +407,13 @@
     right, left = from_right(cosines.T), from_left(cosines)
     back_right, back_left = from_right(cosines), from_left(cosines.T)
     index = indices.reshape(indices.shape[-2:]).T
-    shares, rows = lax.axis_size(DP[0]), lax.axis_size(TENSOR)
-    outgoing, index_rows = pick(gradient, momentum, in_hbm(index), in_hbm(right), in_hbm(left), shares)
+    rows = lax.axis_size(TENSOR)
+    outgoing, index_rows = pick(gradient, momentum, in_hbm(index), in_hbm(right), in_hbm(left), SHARES)
     received = lax.all_to_all(outgoing, DP, split_axis=0, concat_axis=0, tiled=True)
-    shared = combine(in_vmem(received), in_vmem(back_right), in_vmem(back_left), shares)
     new_momentum = remain(gradient, momentum, index_rows, right, left, back_right, back_left)
-    gathered = in_vmem(exchange(shared, gather_lines()))
-    energy = row_total(gathered, in_hbm(new_momentum), rows)
+    shared = combine(in_vmem(received), in_vmem(back_right), in_vmem(back_left), in_hbm(new_momentum), SHARES)
+    gathered = in_vmem(exchange(shared, share_holders(SHARES)))
+    energy = row_total(gathered, rows)
     energies = lax.all_to_all(energy, TENSOR, split_axis=0, concat_axis=0, tiled=True)
     update = scale(gathered, in_vmem(energies), height * columns * rows)
     return (new_momentum[None], update)

time: 72.7 us -> 74.6 us (1.026)
  blocking collectives: 40.4 us -> 25 us
  starting transfers between devices: 3.57 us -> 17.1 us
  Pallas kernels: 18.1 us -> 22 us
  waiting for transfers between devices: 9.62 us -> 8.79 us
    all_to_all x1, blocking collectives: 28.7 us -> 12.1 us  [exchange(): lax.all_to_all(copies, EVERY, split_axis=0, concat_axis=0, axis_index_gro...]
    all_to_all x1, starting transfers between devices: 3.57 us -> 17.1 us  [local(): lax.all_to_all(outgoing, DP, split_axis=0, concat_axis=0, tiled=True)]
    pallas_call x2, Pallas kernels: 3.05 us -> 7.21 us  [the longest x1 7.13 us: combine(): pl.pallas_call(combine_kernel, in_specs=[VMEM] * 3 + [HBM], out_specs=HBM...]
    all_to_all x1, blocking collectives: 11.8 us -> 12.9 us  [local(): lax.all_to_all(energy, TENSOR, split_axis=0, concat_axis=0, tiled=True)]
    all_to_all x1, waiting for transfers between devices: 9.62 us -> 8.79 us  [local(): lax.all_to_all(outgoing, DP, split_axis=0, concat_axis=0, tiled=True)]
where the time goes in v5:
time: 74.6 us; the launch traced here: 74.2 us
  blocking collectives  25 us (34%)
  Pallas kernels  22 us (29%)
  starting transfers between devices  17.1 us (23%)
  waiting for transfers between devices  8.79 us (12%)
    all_to_all x1, starting transfers between devices, local(): lax.all_to_all(outgoing, DP, split_axis=0, concat_axis=0, tiled=True)  17.1 us
    all_to_all x1, blocking collectives, local(): lax.all_to_all(energy, TENSOR, split_axis=0, concat_axis=0, tiled=True)  12.9 us
    all_to_all x1, blocking collectives, exchange(): lax.all_to_all(copies, EVERY, split_axis=0, concat_axis=0, axis_index_gro...  12.1 us
    all_to_all x1, waiting for transfers between devices, local(): lax.all_to_all(outgoing, DP, split_axis=0, concat_axis=0, tiled=True)  8.79 us
    pallas_call x1, Pallas kernels, remain(): pl.pallas_call(functools.partial(remain_kernel, width // LANES), grid=(st...  8.6 us
    pallas_call x1, Pallas kernels, combine(): pl.pallas_call(combine_kernel, in_specs=[VMEM] * 3 + [HBM], out_specs=HBM...  7.13 us
    pallas_call x1, Pallas kernels, pick(): pl.pallas_call(functools.partial(pick_kernel, steps), in_specs=[HBM] * 5,...  5.03 us
  transfers between devices with their start and end apart: 1, of which 1 were waited for; matrix products, arithmetic and copies ran while one was open for 0% of the time, Pallas kernels for 12%

profile of v5, /device:TPU:1, one launch (start us, length us, event | category | flops | bytes accessed | tf_op | source)
XLA Modules:
  0.0 74.2 jit_solution(4915394687685734397)
XLA Ops:
  0.6 5.0 %pick.1 = (bf16[64,32,128]{2,1,0:T(8,128)(2,1)}, f32[64,128]{1,0:T(8,128)S(1)}) custom-call(bf16[64,8192]{1,0:T(8,128)(2,1)} %bitcast.6, bf16[64,8192]{1,0:T(8,128)(2,1)} %bitcast.8, s32[32,128]{1,0:T(8,128)} %bitcast.11, bf16[2,256,256]{2,1,0:T(8,128)(2,1)} %constant.8.clone.right_in.right_ref, bf16[64,192]{1,0:T(8,128)(2,1)} %constant.9.clone.left_in.left_ref), custom_call_target="tpu_custom_call" | custom-call | tf_op jit(solution)/shard_map/pick/pallas_call | solution.py:183
  5.7 0.0 copy-start.2
  5.7 0.6 copy-done.2
  6.3 17.1 %all-to-all-start = ((bf16[64,32,128]{2,1,0:T(8,128)(2,1)}), bf16[64,32,128]{2,1,0:T(8,128)(2,1)S(1)}, u32[]{:S(2)}, u32[]{:S(2)}) async-start(bf16[64,32,128]{2,1,0:T(8,128)(2,1)} %get-tuple-element.5), calls=%async_computation | async-start | bytes 1048576 | tf_op jit(solution)/shard_map/all_to_all | solution.py:412
  23.4 0.0 copy-start
  23.4 0.0 copy-start.1
  23.4 8.6 %remain.1.after_ref = bf16[64,8192]{1,0:T(8,128)(2,1)} custom-call(bf16[64,8192]{1,0:T(8,128)(2,1)} %bitcast.7, bf16[64,8192]{1,0:T(8,128)(2,1)} %bitcast.9, f32[64,128]{1,0:T(8,128)} %copy-done.2, bf16[2,256,256]{2,1,0:T(8,128)(2,1)} %constant.8.clone.right_in.right_ref, bf16[64,192]{1,0:T(8,128)(2,1)} %constant.9.clone.left_in.left_ref, ...), custom_call_target="tpu_custom_call" | custom-call | flops 5000000000 | bytes 3145728 | tf_op jit(solution)/shard_map/remain/pallas_call | solution.py:221
  32.0 8.8 %all-to-all-done.in_ref = bf16[64,32,128]{2,1,0:T(8,128)(2,1)S(1)} async-done(((bf16[64,32,128]{2,1,0:T(8,128)(2,1)}), bf16[64,32,128]{2,1,0:T(8,128)(2,1)S(1)}, u32[]{:S(2)}, u32[]{:S(2)}) %all-to-all-start) | async-done | bytes 524320 | tf_op jit(solution)/shard_map/all_to_all | solution.py:412
  40.8 0.0 copy-done
  40.8 0.0 copy-done.1
  40.8 7.1 %combine.1 = bf16[2,2056,128]{2,1,0:T(8,128)(2,1)} custom-call(bf16[64,32,128]{2,1,0:T(8,128)(2,1)S(1)} %all-to-all-done.in_ref, bf16[2,256,256]{2,1,0:T(8,128)(2,1)S(1)} %copy-done, bf16[64,192]{1,0:T(8,128)(2,1)S(1)} %copy-done.1, bf16[64,8192]{1,0:T(8,128)(2,1)} %remain.1.after_ref), custom_call_target="tpu_custom_call" | custom-call | tf_op jit(solution)/shard_map/combine/pallas_call | solution.py:302
  48.0 12.1 %all_to_all.15.in_ref = bf16[2,2056,128]{2,1,0:T(8,128)(2,1)S(1)} all-to-all(bf16[2,2056,128]{2,1,0:T(8,128)(2,1)} %combine.1), channel_id=1, replica_groups={{0,8},{16,24},{32,40},{48,56},{64,72},{80,88},{96,104},{112,120},{128,1..., dimensions={0} | all-to-all | bytes 2105344 | tf_op jit(solution)/shard_map/all_to_all | solution.py:392
  60.1 0.1 row_total.1
  60.2 12.9 %all_to_all.16.energy_ref = f32[8,8,128]{2,1,0:T(8,128)S(1)} all-to-all(f32[8,8,128]{2,1,0:T(8,128)S(1)} %row_total.1), channel_id=1, replica_groups=mesh['dp_0'=8,'dp_1'=8,'tensor_0'=4,'tensor_1'=2] {'tensor_0','tensor_1'}, dimensions={0} | all-to-all | bytes 65536 | tf_op jit(solution)/shard_map/all_to_all | solution.py:417
  73.1 1.1 %scale.1 = bf16[64,8192]{1,0:T(8,128)(2,1)} custom-call(bf16[2,2056,128]{2,1,0:T(8,128)(2,1)S(1)} %all_to_all.15.in_ref, f32[8,8,128]{2,1,0:T(8,128)S(1)} %all_to_all.16.energy_ref), custom_call_target="tpu_custom_call" | custom-call | tf_op jit(solution)/shard_map/scale/pallas_call | solution.py:366
Async XLA Ops:
  5.7 0.6 copy-start.2
  6.3 34.6 %all-to-all-start = ((bf16[64,32,128]{2,1,0:T(8,128)(2,1)}), bf16[64,32,128]{2,1,0:T(8,128)(2,1)S(1)}, u32[]{:S(2)}, u32[]{:S(2)}) async-start(bf16[64,32,128]{2,1,0:T(8,128)(2,1)} %get-tuple-element.5), calls=%async_computation | async-start | bytes 1048576 | tf_op jit(solution)/shard_map/all_to_all | solution.py:412
  23.4 17.4 %copy-start = (bf16[2,256,256]{2,1,0:T(8,128)(2,1)S(1)}, bf16[2,256,256]{2,1,0:T(8,128)(2,1)}, u32[]{:S(2)}) copy-start(bf16[2,256,256]{2,1,0:T(8,128)(2,1)} %constant.10.clone.back_right_ref.right_ref) | copy-start | bytes 786436
  23.4 17.4 %copy-start.1 = (bf16[64,192]{1,0:T(8,128)(2,1)S(1)}, bf16[64,192]{1,0:T(8,128)(2,1)}, u32[]{:S(2)}) copy-start(bf16[64,192]{1,0:T(8,128)(2,1)} %constant.11.clone.back_left_ref.left_ref) | copy-start | bytes 73732

commit v6 on v5

--- a/solution.py
+++ b/solution.py
@@ -12,7 +12,7 @@
 BLOCK = 64
 LANES = 256
 QUAD = 4
-SHARES = 2
+SHARES = 8
 TENSOR = ("tensor_0", "tensor_1")
 DP = ("dp_0", "dp_1")
 EVERY = DP + TENSOR
@@ -162,7 +162,7 @@
     line = lax.axis_size(DP[1])
     for peer in range(out_ref.shape[0]):
         along_first, along_second = peer // line % shares, peer % line % shares
-        share = along_second + (along_first - along_second) * core
+        share = along_first + (along_second - along_first) * core
         pltpu.make_async_copy(payload_ref.at[share], out_ref.at[peer], sent).start()
     pltpu.make_async_copy(out_ref, out_ref, sent).wait()
 
@@ -229,7 +229,7 @@
     )(gradient, momentum, rows, right, left, back_right, back_left)
 
 
-def combine_kernel(in_ref, right_ref, left_ref, after_ref, out_ref, stage_ref, table_ref, sum_ref, block_ref, stamp_ref, sent):
+def combine_kernel(in_ref, right_ref, left_ref, out_ref, stage_ref, table_ref, sum_ref, block_ref, stamp_ref, sent):
     sources, double, count = in_ref.shape
     groups, selected = double // 2, count // QUAD
     halved = 128 // sources
@@ -295,13 +295,13 @@
     pltpu.make_async_copy(out_ref, out_ref, sent).wait()
 
 
-def combine(received, right, left, after, peers):
+def combine(received, right, left, peers):
     sources, double, count = received.shape
     height = double // 2 * BLOCK
     block = (height * LANES // 128, 128)
     return pl.pallas_call(
         combine_kernel,
-        in_specs=[VMEM] * 3 + [HBM],
+        in_specs=[VMEM] * 3,
         out_specs=HBM,
         out_shape=pltpu.HBM((peers, block[0] + 8, block[1]), BF16),
         scratch_shapes=[
@@ -314,29 +314,28 @@
         ],
         compiler_params=LIMIT,
         name="combine",
-    )(received, right, left, after)
-
-
-def total_kernel(in_ref, out_ref):
+    )(received, right, left)
+
+
+def total_kernel(in_ref, after_ref, out_ref):
     total = jnp.zeros((1, 1), F32)
     for share in range(in_ref.shape[0]):
         total = total + jnp.sum(in_ref[share, in_ref.shape[1] - 8 :, :].astype(F32)[:, :1], axis=0, keepdims=True)
     tile = out_ref.shape[1:]
-    corner = jnp.logical_and(iota(tile, 0, jnp.int32) == 0, iota(tile, 1, jnp.int32) == 0)
-    tile = jnp.where(corner, total, 0.0)
+    tile = jnp.where(iota(tile, 1, jnp.int32) == 0, total, 0.0)
     for peer in range(out_ref.shape[0]):
         out_ref[peer] = tile
 
 
-def row_total(gathered, rows):
+def row_total(gathered, after, rows):
     return pl.pallas_call(
         total_kernel,
-        in_specs=[VMEM],
+        in_specs=[VMEM, HBM],
         out_specs=VMEM,
-        out_shape=pltpu.VMEM((rows, 8, 128), F32),
+        out_shape=pltpu.VMEM((rows, 1, 128), F32),
         compiler_params=LIMIT,
         name="row_total",
-    )(gathered)
+    )(gathered, after)
 
 
 def scale_kernel(count, in_ref, energy_ref, out_ref, scaled_ref, stored):
@@ -383,8 +382,8 @@
     place = places()
     groups = []
     for chip in range(place.shape[2]):
-        groups.extend(place[:, :, chip, 0].reshape(-1, shares).tolist())
-        groups.extend(place[:, :, chip, 1].T.reshape(-1, shares).tolist())
+        groups.extend(place[:, :, chip, 0].T.reshape(-1, shares).tolist())
+        groups.extend(place[:, :, chip, 1].reshape(-1, shares).tolist())
     return groups
 
 
@@ -410,10 +409,10 @@
     rows = lax.axis_size(TENSOR)
     outgoing, index_rows = pick(gradient, momentum, in_hbm(index), in_hbm(right), in_hbm(left), SHARES)
     received = lax.all_to_all(outgoing, DP, split_axis=0, concat_axis=0, tiled=True)
+    shared = combine(in_vmem(received), in_vmem(back_right), in_vmem(back_left), SHARES)
     new_momentum = remain(gradient, momentum, index_rows, right, left, back_right, back_left)
-    shared = combine(in_vmem(received), in_vmem(back_right), in_vmem(back_left), in_hbm(new_momentum), SHARES)
     gathered = in_vmem(exchange(shared, share_holders(SHARES)))
-    energy = row_total(gathered, rows)
+    energy = row_total(gathered, in_hbm(new_momentum), rows)
     energies = lax.all_to_all(energy, TENSOR, split_axis=0, concat_axis=0, tiled=True)
     update = scale(gathered, in_vmem(energies), height * columns * rows)
     return (new_momentum[None], update)

time: 74.6 us -> 72.3 us (0.969)
  blocking collectives: 25 us -> 40.3 us
  starting transfers between devices: 17.1 us -> 3.57 us
  Pallas kernels: 22 us -> 17.8 us
  waiting for transfers between devices: 8.79 us -> 9.62 us
    all_to_all x1, blocking collectives: 12.1 us -> 28.7 us  [local(): lax.all_to_all(outgoing, DP, split_axis=0, concat_axis=0, tiled=True)]
    all_to_all x1, starting transfers between devices: 17.1 us -> 3.57 us  [exchange(): lax.all_to_all(copies, EVERY, split_axis=0, concat_axis=0, axis_index_gro...]
    pallas_call x2, Pallas kernels: 7.21 us -> 3.05 us  [the longest x1 2.96 us: combine(): pl.pallas_call(combine_kernel, in_specs=[VMEM] * 3, out_specs=HBM, out_sh...]
    all_to_all x1, blocking collectives: 12.9 us -> 11.7 us  [local(): lax.all_to_all(energy, TENSOR, split_axis=0, concat_axis=0, tiled=True)]
    all_to_all x1, waiting for transfers between devices: 8.79 us -> 9.62 us  [exchange(): lax.all_to_all(copies, EVERY, split_axis=0, concat_axis=0, axis_index_gro...]
where the time goes in v6:
time: 72.3 us; the launch traced here: 72.1 us
  blocking collectives  40.3 us (56%)
  Pallas kernels  17.8 us (25%)
  waiting for transfers between devices  9.62 us (13%)
  starting transfers between devices  3.57 us (5%)
    all_to_all x1, blocking collectives, local(): lax.all_to_all(outgoing, DP, split_axis=0, concat_axis=0, tiled=True)  28.7 us
    all_to_all x1, blocking collectives, local(): lax.all_to_all(energy, TENSOR, split_axis=0, concat_axis=0, tiled=True)  11.7 us
    all_to_all x1, waiting for transfers between devices, exchange(): lax.all_to_all(copies, EVERY, split_axis=0, concat_axis=0, axis_index_gro...  9.62 us
    pallas_call x1, Pallas kernels, remain(): pl.pallas_call(functools.partial(remain_kernel, width // LANES), grid=(st...  8.57 us
    pallas_call x1, Pallas kernels, pick(): pl.pallas_call(functools.partial(pick_kernel, steps), in_specs=[HBM] * 5,...  5.05 us
    all_to_all x1, starting transfers between devices, exchange(): lax.all_to_all(copies, EVERY, split_axis=0, concat_axis=0, axis_index_gro...  3.57 us
    pallas_call x1, Pallas kernels, combine(): pl.pallas_call(combine_kernel, in_specs=[VMEM] * 3, out_specs=HBM, out_sh...  2.96 us
  transfers between devices with their start and end apart: 1, of which 1 were waited for; matrix products, arithmetic and copies ran while one was open for 0% of the time, Pallas kernels for 12%

profile of v6, /device:TPU:1, one launch (start us, length us, event | category | flops | bytes accessed | tf_op | source)
XLA Modules:
  0.0 72.1 jit_solution(15637034218495047410)
XLA Ops:
  0.6 0.0 copy-start
  0.6 0.0 copy-start.1
  0.7 5.0 %pick.1 = (bf16[64,8,128]{2,1,0:T(8,128)(2,1)}, f32[64,128]{1,0:T(8,128)S(1)}) custom-call(bf16[64,8192]{1,0:T(8,128)(2,1)} %bitcast.6, bf16[64,8192]{1,0:T(8,128)(2,1)} %bitcast.8, s32[32,128]{1,0:T(8,128)} %bitcast.11, bf16[2,256,256]{2,1,0:T(8,128)(2,1)} %constant.8.clone.right_in.right_ref, bf16[64,192]{1,0:T(8,128)(2,1)} %constant.9.clone.left_in.left_ref), custom_call_target="tpu_custom_call" | custom-call | tf_op jit(solution)/shard_map/pick/pallas_call | solution.py:183
  5.7 0.0 copy-start.2
  5.7 28.7 %all_to_all.15.in_ref = bf16[64,8,128]{2,1,0:T(8,128)(2,1)S(1)} all-to-all(bf16[64,8,128]{2,1,0:T(8,128)(2,1)} %get-tuple-element.5), channel_id=1, replica_groups=mesh['dp_0'=8,'dp_1'=8,'tensor_0'=4,'tensor_1'=2] {'dp_0','dp_1'}, dimensions={0} | all-to-all | bytes 262144 | tf_op jit(solution)/shard_map/all_to_all | solution.py:411
  34.4 0.0 copy-done
  34.4 0.0 copy-done.1
  34.4 3.0 %combine.1 = bf16[8,520,128]{2,1,0:T(8,128)(2,1)} custom-call(bf16[64,8,128]{2,1,0:T(8,128)(2,1)S(1)} %all_to_all.15.in_ref, bf16[2,256,256]{2,1,0:T(8,128)(2,1)S(1)} %copy-done, bf16[64,192]{1,0:T(8,128)(2,1)S(1)} %copy-done.1), custom_call_target="tpu_custom_call" | custom-call | tf_op jit(solution)/shard_map/combine/pallas_call | solution.py:302
  37.4 0.0 copy-done.2
  37.4 3.6 %all-to-all-start.1 = ((bf16[8,520,128]{2,1,0:T(8,128)(2,1)}), bf16[8,520,128]{2,1,0:T(8,128)(2,1)S(1)}, u32[]{:S(2)}, u32[]{:S(2)}) async-start(bf16[8,520,128]{2,1,0:T(8,128)(2,1)} %combine.1), calls=%async_computation.1 | async-start | bytes 2129920 | tf_op jit(solution)/shard_map/all_to_all | solution.py:391
  41.0 8.6 %remain.1.after_ref = bf16[64,8192]{1,0:T(8,128)(2,1)} custom-call(bf16[64,8192]{1,0:T(8,128)(2,1)} %bitcast.7, bf16[64,8192]{1,0:T(8,128)(2,1)} %bitcast.9, f32[64,128]{1,0:T(8,128)} %copy-done.2, bf16[2,256,256]{2,1,0:T(8,128)(2,1)} %constant.8.clone.right_in.right_ref, bf16[64,192]{1,0:T(8,128)(2,1)} %constant.9.clone.left_in.left_ref, ...), custom_call_target="tpu_custom_call" | custom-call | flops 5000000000 | bytes 3145728 | tf_op jit(solution)/shard_map/remain/pallas_call | solution.py:221
  49.5 9.6 %all-to-all-done.1.in_ref = bf16[8,520,128]{2,1,0:T(8,128)(2,1)S(1)} async-done(((bf16[8,520,128]{2,1,0:T(8,128)(2,1)}), bf16[8,520,128]{2,1,0:T(8,128)(2,1)S(1)}, u32[]{:S(2)}, u32[]{:S(2)}) %all-to-all-start.1) | async-done | bytes 1064992 | tf_op jit(solution)/shard_map/all_to_all | solution.py:391
  59.1 0.1 row_total.1
  59.2 11.7 %all_to_all.16.energy_ref = f32[8,1,128]{2,1,0:T(1,128)S(1)} all-to-all(f32[8,1,128]{2,1,0:T(1,128)S(1)} %row_total.1), channel_id=1, replica_groups=mesh['dp_0'=8,'dp_1'=8,'tensor_0'=4,'tensor_1'=2] {'tensor_0','tensor_1'}, dimensions={0} | all-to-all | bytes 8192 | tf_op jit(solution)/shard_map/all_to_all | solution.py:416
  70.9 1.1 %scale.1 = bf16[64,8192]{1,0:T(8,128)(2,1)} custom-call(bf16[8,520,128]{2,1,0:T(8,128)(2,1)S(1)} %all-to-all-done.1.in_ref, f32[8,1,128]{2,1,0:T(1,128)S(1)} %all_to_all.16.energy_ref), custom_call_target="tpu_custom_call" | custom-call | tf_op jit(solution)/shard_map/scale/pallas_call | solution.py:365
Async XLA Ops:
  0.6 33.8 %copy-start = (bf16[2,256,256]{2,1,0:T(8,128)(2,1)S(1)}, bf16[2,256,256]{2,1,0:T(8,128)(2,1)}, u32[]{:S(2)}) copy-start(bf16[2,256,256]{2,1,0:T(8,128)(2,1)} %constant.10.clone.back_right_ref.right_ref) | copy-start | bytes 786436
  0.6 33.8 %copy-start.1 = (bf16[64,192]{1,0:T(8,128)(2,1)S(1)}, bf16[64,192]{1,0:T(8,128)(2,1)}, u32[]{:S(2)}) copy-start(bf16[64,192]{1,0:T(8,128)(2,1)} %constant.11.clone.back_left_ref.left_ref) | copy-start | bytes 73732
  5.7 31.7 %copy-start.2 = (f32[64,128]{1,0:T(8,128)}, f32[64,128]{1,0:T(8,128)S(1)}, u32[]{:S(2)}) copy-start(f32[64,128]{1,0:T(8,128)S(1)} %get-tuple-element.4.rows_ref) | copy-start | bytes 98308
  37.4 21.8 %all-to-all-start.1 = ((bf16[8,520,128]{2,1,0:T(8,128)(2,1)}), bf16[8,520,128]{2,1,0:T(8,128)(2,1)S(1)}, u32[]{:S(2)}, u32[]{:S(2)}) async-start(bf16[8,520,128]{2,1,0:T(8,128)(2,1)} %combine.1), calls=%async_computation.1 | async-start | bytes 2129920 | tf_op jit(solution)/shard_map/all_to_all | solution.py:391

commit v7 on v6

--- a/solution.py
+++ b/solution.py
@@ -111,7 +111,7 @@
 
 def pick_kernel(
     steps, gradient_in, momentum_in, index_in, right_in, left_in, out_ref, rows_ref,
-    gradient_ref, momentum_ref, index_ref, right_ref, left_ref, payload_ref, loaded, sent
+    gradient_ref, momentum_ref, index_ref, right_ref, left_ref, payload_ref, loaded
 ):
     starts = np.cumsum([0, *steps])
     tables = [
@@ -162,9 +162,7 @@
     line = lax.axis_size(DP[1])
     for peer in range(out_ref.shape[0]):
         along_first, along_second = peer // line % shares, peer % line % shares
-        share = along_first + (along_second - along_first) * core
-        pltpu.make_async_copy(payload_ref.at[share], out_ref.at[peer], sent).start()
-    pltpu.make_async_copy(out_ref, out_ref, sent).wait()
+        out_ref[peer] = payload_ref[along_first + (along_second - along_first) * core]
 
 
 VMEM = pl.BlockSpec(memory_space=pltpu.VMEM)
@@ -183,8 +181,8 @@
     return pl.pallas_call(
         functools.partial(pick_kernel, steps),
         in_specs=[HBM] * 5,
-        out_specs=[HBM, VMEM],
-        out_shape=[pltpu.HBM((lax.axis_size(DP), *share_shape), BF16), pltpu.VMEM((2 * groups, count), F32)],
+        out_specs=[VMEM, VMEM],
+        out_shape=[pltpu.VMEM((lax.axis_size(DP), *share_shape), BF16), pltpu.VMEM((2 * groups, count), F32)],
         scratch_shapes=[
             pltpu.VMEM(gradient.shape, BF16),
             pltpu.VMEM(momentum.shape, BF16),
@@ -193,7 +191,6 @@
             pltpu.VMEM(left.shape, BF16),
             pltpu.VMEM((shares, *share_shape), BF16),
             pltpu.SemaphoreType.DMA((2 * len(steps) + 3,)),
-            pltpu.SemaphoreType.DMA,
         ],
         name="pick",
     )(gradient, momentum, index, right, left)
@@ -273,15 +270,19 @@
                 energy = energy + square[r : r + 8]
             parts.append(total)
         sum_ref[g * BLOCK : (g + 1) * BLOCK, :] = jnp.concatenate(parts, axis=1)
-    half = times_right(sum_ref[...], right_ref)
-    for g in range(groups):
-        tile = times_left(left_ref, half[g * BLOCK : (g + 1) * BLOCK]).astype(BF16)
-        for k in range(LANES // 128):
-            at = (g * (LANES // 128) + k) * BLOCK
-            block_ref[at : at + BLOCK, :] = tile[:, k * 128 : (k + 1) * 128]
+    height = BLOCK * (LANES // 128)
+    batch = groups // 2
+    for first in range(0, groups, batch):
+        half = times_right(sum_ref[first * BLOCK : (first + batch) * BLOCK, :], right_ref)
+        for g in range(batch):
+            tile = times_left(left_ref, half[g * BLOCK : (g + 1) * BLOCK]).astype(BF16)
+            for k in range(LANES // 128):
+                at = (first + g) * height + k * BLOCK
+                block_ref[at : at + BLOCK, :] = tile[:, k * 128 : (k + 1) * 128]
+        part = pl.ds(first * height, batch * height)
+        for peer in range(out_ref.shape[0]):
+            pltpu.make_async_copy(block_ref.at[part], out_ref.at[peer, part], sent).start()
     height = block_ref.shape[0]
-    for peer in range(out_ref.shape[0]):
-        pltpu.make_async_copy(block_ref, out_ref.at[peer, pl.ds(0, height)], sent).start()
     total = jnp.sum(jnp.sum(energy, axis=0, keepdims=True), axis=1, keepdims=True)
     at = iota(stamp_ref.shape, 0, jnp.int32)
     stamp = jnp.zeros(stamp_ref.shape, F32)

time: 72.3 us -> 71.2 us (0.985)
  Pallas kernels: 17.8 us -> 16.9 us
    pallas_call x1, Pallas kernels: 5.05 us -> 4.26 us  [pick(): pl.pallas_call(functools.partial(pick_kernel, steps), in_specs=[HBM] * 5,...]
where the time goes in v7:
time: 71.2 us; the launch traced here: 70.9 us
  blocking collectives  40.1 us (56%)
  Pallas kernels  16.9 us (24%)
  waiting for transfers between devices  9.63 us (14%)
  starting transfers between devices  3.57 us (5%)
    all_to_all x1, blocking collectives, local(): lax.all_to_all(outgoing, DP, split_axis=0, concat_axis=0, tiled=True)  28.5 us
    all_to_all x1, blocking collectives, local(): lax.all_to_all(energy, TENSOR, split_axis=0, concat_axis=0, tiled=True)  11.7 us
    all_to_all x1, waiting for transfers between devices, exchange(): lax.all_to_all(copies, EVERY, split_axis=0, concat_axis=0, axis_index_gro...  9.63 us
    pallas_call x1, Pallas kernels, remain(): pl.pallas_call(functools.partial(remain_kernel, width // LANES), grid=(st...  8.56 us
    pallas_call x1, Pallas kernels, pick(): pl.pallas_call(functools.partial(pick_kernel, steps), in_specs=[HBM] * 5,...  4.26 us
    all_to_all x1, starting transfers between devices, exchange(): lax.all_to_all(copies, EVERY, split_axis=0, concat_axis=0, axis_index_gro...  3.57 us
    pallas_call x1, Pallas kernels, combine(): pl.pallas_call(combine_kernel, in_specs=[VMEM] * 3, out_specs=HBM, out_sh...  2.84 us
  transfers between devices with their start and end apart: 1, of which 1 were waited for; matrix products, arithmetic and copies ran while one was open for 0% of the time, Pallas kernels for 12%

profile of v7, /device:TPU:1, one launch (start us, length us, event | category | flops | bytes accessed | tf_op | source)
XLA Modules:
  0.0 70.9 jit_solution(17963070225400175798)
XLA Ops:
  0.6 0.0 copy-start
  0.6 0.0 copy-start.1
  0.7 4.3 %pick.1 = (bf16[64,8,128]{2,1,0:T(8,128)(2,1)S(1)}, f32[64,128]{1,0:T(8,128)S(1)}) custom-call(bf16[64,8192]{1,0:T(8,128)(2,1)} %bitcast.6, bf16[64,8192]{1,0:T(8,128)(2,1)} %bitcast.8, s32[32,128]{1,0:T(8,128)} %bitcast.11, bf16[2,256,256]{2,1,0:T(8,128)(2,1)} %constant.8.clone.right_in.right_ref, bf16[64,192]{1,0:T(8,128)(2,1)} %constant.9.clone.left_in.left_ref), custom_call_target="tpu_custom_call" | custom-call | tf_op jit(solution)/shard_map/pick/pallas_call | solution.py:181
  4.9 0.0 copy-start.2
  4.9 28.5 %all_to_all.15.in_ref = bf16[64,8,128]{2,1,0:T(8,128)(2,1)S(1)} all-to-all(bf16[64,8,128]{2,1,0:T(8,128)(2,1)S(1)} %get-tuple-element.5), channel_id=1, replica_groups=mesh['dp_0'=8,'dp_1'=8,'tensor_0'=4,'tensor_1'=2] {'dp_0','dp_1'}, dimensions={0} | all-to-all | bytes 262144 | tf_op jit(solution)/shard_map/all_to_all | solution.py:412
  33.4 0.0 copy-done
  33.4 0.0 copy-done.1
  33.4 2.8 %combine.1 = bf16[8,520,128]{2,1,0:T(8,128)(2,1)} custom-call(bf16[64,8,128]{2,1,0:T(8,128)(2,1)S(1)} %all_to_all.15.in_ref, bf16[2,256,256]{2,1,0:T(8,128)(2,1)S(1)} %copy-done, bf16[64,192]{1,0:T(8,128)(2,1)S(1)} %copy-done.1), custom_call_target="tpu_custom_call" | custom-call | tf_op jit(solution)/shard_map/combine/pallas_call | solution.py:303
  36.2 0.0 copy-done.2
  36.3 3.6 %all-to-all-start.1 = ((bf16[8,520,128]{2,1,0:T(8,128)(2,1)}), bf16[8,520,128]{2,1,0:T(8,128)(2,1)S(1)}, u32[]{:S(2)}, u32[]{:S(2)}) async-start(bf16[8,520,128]{2,1,0:T(8,128)(2,1)} %combine.1), calls=%async_computation.1 | async-start | bytes 2129920 | tf_op jit(solution)/shard_map/all_to_all | solution.py:392
  39.8 8.6 %remain.1.after_ref = bf16[64,8192]{1,0:T(8,128)(2,1)} custom-call(bf16[64,8192]{1,0:T(8,128)(2,1)} %bitcast.7, bf16[64,8192]{1,0:T(8,128)(2,1)} %bitcast.9, f32[64,128]{1,0:T(8,128)} %copy-done.2, bf16[2,256,256]{2,1,0:T(8,128)(2,1)} %constant.8.clone.right_in.right_ref, bf16[64,192]{1,0:T(8,128)(2,1)} %constant.9.clone.left_in.left_ref, ...), custom_call_target="tpu_custom_call" | custom-call | flops 5000000000 | bytes 3145728 | tf_op jit(solution)/shard_map/remain/pallas_call | solution.py:218
  48.4 9.6 %all-to-all-done.1.in_ref = bf16[8,520,128]{2,1,0:T(8,128)(2,1)S(1)} async-done(((bf16[8,520,128]{2,1,0:T(8,128)(2,1)}), bf16[8,520,128]{2,1,0:T(8,128)(2,1)S(1)}, u32[]{:S(2)}, u32[]{:S(2)}) %all-to-all-start.1) | async-done | bytes 1064992 | tf_op jit(solution)/shard_map/all_to_all | solution.py:392
  58.0 0.1 row_total.1
  58.1 11.7 %all_to_all.16.energy_ref = f32[8,1,128]{2,1,0:T(1,128)S(1)} all-to-all(f32[8,1,128]{2,1,0:T(1,128)S(1)} %row_total.1), channel_id=1, replica_groups=mesh['dp_0'=8,'dp_1'=8,'tensor_0'=4,'tensor_1'=2] {'tensor_0','tensor_1'}, dimensions={0} | all-to-all | bytes 8192 | tf_op jit(solution)/shard_map/all_to_all | solution.py:417
  69.8 1.1 %scale.1 = bf16[64,8192]{1,0:T(8,128)(2,1)} custom-call(bf16[8,520,128]{2,1,0:T(8,128)(2,1)S(1)} %all-to-all-done.1.in_ref, f32[8,1,128]{2,1,0:T(1,128)S(1)} %all_to_all.16.energy_ref), custom_call_target="tpu_custom_call" | custom-call | tf_op jit(solution)/shard_map/scale/pallas_call | solution.py:366
Async XLA Ops:
  0.6 32.8 %copy-start = (bf16[2,256,256]{2,1,0:T(8,128)(2,1)S(1)}, bf16[2,256,256]{2,1,0:T(8,128)(2,1)}, u32[]{:S(2)}) copy-start(bf16[2,256,256]{2,1,0:T(8,128)(2,1)} %constant.10.clone.back_right_ref.right_ref) | copy-start | bytes 786436
  0.6 32.8 %copy-start.1 = (bf16[64,192]{1,0:T(8,128)(2,1)S(1)}, bf16[64,192]{1,0:T(8,128)(2,1)}, u32[]{:S(2)}) copy-start(bf16[64,192]{1,0:T(8,128)(2,1)} %constant.11.clone.back_left_ref.left_ref) | copy-start | bytes 73732
  4.9 31.3 %copy-start.2 = (f32[64,128]{1,0:T(8,128)}, f32[64,128]{1,0:T(8,128)S(1)}, u32[]{:S(2)}) copy-start(f32[64,128]{1,0:T(8,128)S(1)} %get-tuple-element.4.rows_ref) | copy-start | bytes 98308
  36.3 21.8 %all-to-all-start.1 = ((bf16[8,520,128]{2,1,0:T(8,128)(2,1)}), bf16[8,520,128]{2,1,0:T(8,128)(2,1)S(1)}, u32[]{:S(2)}, u32[]{:S(2)}) async-start(bf16[8,520,128]{2,1,0:T(8,128)(2,1)} %combine.1), calls=%async_computation.1 | async-start | bytes 2129920 | tf_op jit(solution)/shard_map/all_to_all | solution.py:392

commit v8 on v7

--- a/solution.py
+++ b/solution.py
@@ -41,7 +41,8 @@
 
 
 def from_right(cosines):
-    return jnp.asarray(np.stack(constant_halves(np.kron(np.eye(QUAD, dtype=np.float32), cosines))))
+    high, low = constant_halves(np.kron(np.eye(QUAD // 2, dtype=np.float32), cosines))
+    return jnp.asarray(np.block([[high, low], [high, np.zeros_like(high)]]))
 
 
 def halves(x):
@@ -58,8 +59,13 @@
 
 
 def times_right(tiles, right_ref):
-    high, low = halves(tiles)
-    return dot(high, right_ref[0]) + dot(low, right_ref[0]) + dot(high, right_ref[1])
+    wide = LANES // 2
+    cuts = [tiles[:, k * wide : (k + 1) * wide] for k in range(2)]
+    both = jnp.concatenate([jnp.concatenate(halves(cut), axis=1) for cut in cuts], axis=0)
+    product = dot(both, right_ref[...])
+    product = product[:, :wide] + product[:, wide:]
+    height = tiles.shape[0]
+    return jnp.concatenate([product[:height], product[height:]], axis=1)
 
 
 def times_left(left_ref, tile):

time: 71.2 us -> 70.6 us (level)
  Pallas kernels: 16.9 us -> 14.9 us
  waiting for transfers between devices: 9.63 us -> 11.1 us
    pallas_call x1, Pallas kernels: 8.56 us -> 7.13 us  [remain(): pl.pallas_call(functools.partial(remain_kernel, width // LANES), grid=(st...]
    all_to_all x1, waiting for transfers between devices: 9.63 us -> 11.1 us  [exchange(): lax.all_to_all(copies, EVERY, split_axis=0, concat_axis=0, axis_index_gro...]
  transfers between devices with their start and end apart: 1 -> 1, of which waited for: 1 -> 1; matrix products, arithmetic and copies ran while one was open for 0% -> 0% of each run, Pallas kernels for 12% -> 10%
where the time goes in v8:
time: 70.6 us; the launch traced here: 70.3 us
  blocking collectives  40.1 us (57%)
  Pallas kernels  14.9 us (21%)
  waiting for transfers between devices  11.1 us (16%)
  starting transfers between devices  3.57 us (5%)
    all_to_all x1, blocking collectives, local(): lax.all_to_all(outgoing, DP, split_axis=0, concat_axis=0, tiled=True)  28.5 us
    all_to_all x1, blocking collectives, local(): lax.all_to_all(energy, TENSOR, split_axis=0, concat_axis=0, tiled=True)  11.7 us
    all_to_all x1, waiting for transfers between devices, exchange(): lax.all_to_all(copies, EVERY, split_axis=0, concat_axis=0, axis_index_gro...  11.1 us
    pallas_call x1, Pallas kernels, remain(): pl.pallas_call(functools.partial(remain_kernel, width // LANES), grid=(st...  7.13 us
    pallas_call x1, Pallas kernels, pick(): pl.pallas_call(functools.partial(pick_kernel, steps), in_specs=[HBM] * 5,...  3.74 us
    all_to_all x1, starting transfers between devices, exchange(): lax.all_to_all(copies, EVERY, split_axis=0, concat_axis=0, axis_index_gro...  3.57 us
    pallas_call x1, Pallas kernels, combine(): pl.pallas_call(combine_kernel, in_specs=[VMEM] * 3, out_specs=HBM, out_sh...  2.77 us
  transfers between devices with their start and end apart: 1, of which 1 were waited for; matrix products, arithmetic and copies ran while one was open for 0% of the time, Pallas kernels for 10%

profile of v8, /device:TPU:1, one launch (start us, length us, event | category | flops | bytes accessed | tf_op | source)
XLA Modules:
  0.0 70.3 jit_solution(6244302415456531784)
XLA Ops:
  0.6 0.0 copy-start
  0.6 0.0 copy-start.1
  0.7 3.7 %pick.1 = (bf16[64,8,128]{2,1,0:T(8,128)(2,1)S(1)}, f32[64,128]{1,0:T(8,128)S(1)}) custom-call(bf16[64,8192]{1,0:T(8,128)(2,1)} %bitcast.6, bf16[64,8192]{1,0:T(8,128)(2,1)} %bitcast.8, s32[32,128]{1,0:T(8,128)} %bitcast.11, bf16[256,256]{1,0:T(8,128)(2,1)} %constant.8.clone.right_in.right_ref, bf16[64,192]{1,0:T(8,128)(2,1)} %constant.9.clone.left_in.left_ref), custom_call_target="tpu_custom_call" | custom-call | tf_op jit(solution)/shard_map/pick/pallas_call | solution.py:187
  4.4 0.0 copy-start.2
  4.4 28.5 %all_to_all.15.in_ref = bf16[64,8,128]{2,1,0:T(8,128)(2,1)S(1)} all-to-all(bf16[64,8,128]{2,1,0:T(8,128)(2,1)S(1)} %get-tuple-element.5), channel_id=1, replica_groups=mesh['dp_0'=8,'dp_1'=8,'tensor_0'=4,'tensor_1'=2] {'dp_0','dp_1'}, dimensions={0} | all-to-all | bytes 262144 | tf_op jit(solution)/shard_map/all_to_all | solution.py:418
  32.9 0.0 copy-done
  32.9 0.0 copy-done.1
  32.9 2.8 %combine.1 = bf16[8,520,128]{2,1,0:T(8,128)(2,1)} custom-call(bf16[64,8,128]{2,1,0:T(8,128)(2,1)S(1)} %all_to_all.15.in_ref, bf16[256,256]{1,0:T(8,128)(2,1)S(1)} %copy-done, bf16[64,192]{1,0:T(8,128)(2,1)S(1)} %copy-done.1), custom_call_target="tpu_custom_call" | custom-call | tf_op jit(solution)/shard_map/combine/pallas_call | solution.py:309
  35.7 0.0 copy-done.2
  35.7 3.6 %all-to-all-start.1 = ((bf16[8,520,128]{2,1,0:T(8,128)(2,1)}), bf16[8,520,128]{2,1,0:T(8,128)(2,1)S(1)}, u32[]{:S(2)}, u32[]{:S(2)}) async-start(bf16[8,520,128]{2,1,0:T(8,128)(2,1)} %combine.1), calls=%async_computation.1 | async-start | bytes 2129920 | tf_op jit(solution)/shard_map/all_to_all | solution.py:398
  39.2 7.1 %remain.1.after_ref = bf16[64,8192]{1,0:T(8,128)(2,1)} custom-call(bf16[64,8192]{1,0:T(8,128)(2,1)} %bitcast.7, bf16[64,8192]{1,0:T(8,128)(2,1)} %bitcast.9, f32[64,128]{1,0:T(8,128)} %copy-done.2, bf16[256,256]{1,0:T(8,128)(2,1)} %constant.8.clone.right_in.right_ref, bf16[64,192]{1,0:T(8,128)(2,1)} %constant.9.clone.left_in.left_ref, ...), custom_call_target="tpu_custom_call" | custom-call | flops 5000000000 | bytes 3145728 | tf_op jit(solution)/shard_map/remain/pallas_call | solution.py:224
  46.4 11.1 %all-to-all-done.1.in_ref = bf16[8,520,128]{2,1,0:T(8,128)(2,1)S(1)} async-done(((bf16[8,520,128]{2,1,0:T(8,128)(2,1)}), bf16[8,520,128]{2,1,0:T(8,128)(2,1)S(1)}, u32[]{:S(2)}, u32[]{:S(2)}) %all-to-all-start.1) | async-done | bytes 1064992 | tf_op jit(solution)/shard_map/all_to_all | solution.py:398
  57.4 0.1 row_total.1
  57.5 11.7 %all_to_all.16.energy_ref = f32[8,1,128]{2,1,0:T(1,128)S(1)} all-to-all(f32[8,1,128]{2,1,0:T(1,128)S(1)} %row_total.1), channel_id=1, replica_groups=mesh['dp_0'=8,'dp_1'=8,'tensor_0'=4,'tensor_1'=2] {'tensor_0','tensor_1'}, dimensions={0} | all-to-all | bytes 8192 | tf_op jit(solution)/shard_map/all_to_all | solution.py:423
  69.2 1.1 %scale.1 = bf16[64,8192]{1,0:T(8,128)(2,1)} custom-call(bf16[8,520,128]{2,1,0:T(8,128)(2,1)S(1)} %all-to-all-done.1.in_ref, f32[8,1,128]{2,1,0:T(1,128)S(1)} %all_to_all.16.energy_ref), custom_call_target="tpu_custom_call" | custom-call | tf_op jit(solution)/shard_map/scale/pallas_call | solution.py:372
Async XLA Ops:
  0.6 32.2 %copy-start = (bf16[256,256]{1,0:T(8,128)(2,1)S(1)}, bf16[256,256]{1,0:T(8,128)(2,1)}, u32[]{:S(2)}) copy-start(bf16[256,256]{1,0:T(8,128)(2,1)} %constant.10.clone.back_right_ref.right_ref) | copy-start | bytes 393220
  0.6 32.2 %copy-start.1 = (bf16[64,192]{1,0:T(8,128)(2,1)S(1)}, bf16[64,192]{1,0:T(8,128)(2,1)}, u32[]{:S(2)}) copy-start(bf16[64,192]{1,0:T(8,128)(2,1)} %constant.11.clone.back_left_ref.left_ref) | copy-start | bytes 73732
  4.4 31.3 %copy-start.2 = (f32[64,128]{1,0:T(8,128)}, f32[64,128]{1,0:T(8,128)S(1)}, u32[]{:S(2)}) copy-start(f32[64,128]{1,0:T(8,128)S(1)} %get-tuple-element.4.rows_ref) | copy-start | bytes 98308
  35.7 21.8 %all-to-all-start.1 = ((bf16[8,520,128]{2,1,0:T(8,128)(2,1)}), bf16[8,520,128]{2,1,0:T(8,128)(2,1)S(1)}, u32[]{:S(2)}, u32[]{:S(2)}) async-start(bf16[8,520,128]{2,1,0:T(8,128)(2,1)} %combine.1), calls=%async_computation.1 | async-start | bytes 2129920 | tf_op jit(solution)/shard_map/all_to_all | solution.py:398
